TPU v7x, 32 devices: a whole 2x2x4 slice. The times are simulated.
32 devices in a mesh: dp: 2 (over x), tp: 4 (over z), sq: 4 (over y, core).
Axes of the slice: x: 2, y: 2, z: 4, core: 2. Of those that a mesh axis runs over, the one named last changes fastest.
Arguments:
- hidden: bfloat16 [512, 6144], P('dp'), parts along dimension 0
- cache_lens: int32 [512], P('dp'), parts along dimension 0
- k_cache: bfloat16 [512, 1024, 128], P('dp', 'sq'), parts along dimension 0
- v_cache: bfloat16 [512, 1024, 128], P('dp', 'sq'), parts along dimension 0
- ln_gain: float32 [6144], replicated
- ln_bias: float32 [6144], replicated
- w_query: bfloat16 [6144, 6144], P(None, 'tp')
- b_query: float32 [6144], P('tp')
- w_kv: bfloat16 [6144, 256], replicated
- b_kv: float32 [256], replicated
- w_out: bfloat16 [6144, 6144], P('tp')
- b_out: float32 [6144], replicated
Outputs:
- output 1: bfloat16 [512, 6144], P('dp'), parts along dimension 0
- output 2: bfloat16 [512, 1024, 128], P('dp', 'sq'), parts along dimension 0
- output 3: bfloat16 [512, 1024, 128], P('dp', 'sq'), parts along dimension 0
There are 2 independent parts. A program takes and returns all parts, laid end to end along the dimension named above; an argument that names none is the same for every part.
All inputs are finite; a program needn't handle non-finite values.
Results may differ from a plain program's by a relative error of at most 0.00351117.
Values sent between devices are 32-bit elements.
A program may use at most 1 GiB of HBM per device.

v0:
```python
import jax
import jax.numpy as jnp
from jax import lax
from jax.sharding import PartitionSpec as P


def layer_norm(x_rows, ln_gain, ln_bias):
    x_wide = x_rows.astype(jnp.float32)
    mean_val = jnp.mean(x_wide, axis=-1, keepdims=True)
    centered = x_wide - mean_val
    variance = jnp.mean(centered * centered, axis=-1, keepdims=True)
    normed = centered * lax.rsqrt(variance + 1e-5)
    return (normed * ln_gain + ln_bias).astype(jnp.bfloat16)


def solution(mesh):
    def local_step(hidden, cache_lens, k_cache, v_cache, ln_gain, ln_bias, w_query, b_query, w_kv, b_kv, w_out, b_out):
        batch, pos_local, head_dim = k_cache.shape
        heads_local = w_query.shape[1] // head_dim
        normed = layer_norm(hidden, ln_gain, ln_bias)
        query = (jnp.dot(normed, w_query, preferred_element_type=jnp.float32) + b_query).astype(jnp.bfloat16)
        query = query.reshape(batch, heads_local, head_dim)
        key_val = (jnp.dot(normed, w_kv, preferred_element_type=jnp.float32) + b_kv).astype(jnp.bfloat16)
        first_pos = lax.axis_index("sq") * pos_local
        positions = first_pos + lax.broadcasted_iota(jnp.int32, (1, pos_local), 1)
        at_slot = (positions == cache_lens[:, None])[:, :, None]
        key_new = jnp.where(at_slot, key_val[:, None, :head_dim], k_cache)
        val_new = jnp.where(at_slot, key_val[:, None, head_dim:], v_cache)
        scores = jnp.einsum("bnd,btd->bnt", query, key_new, preferred_element_type=jnp.float32) * (head_dim ** -0.5)
        valid = (positions <= cache_lens[:, None])[:, None, :]
        scores = jnp.where(valid, scores, -1e30)
        local_max = jnp.max(scores, axis=-1, keepdims=True)
        global_max = lax.pmax(local_max, "sq")
        weights = jnp.where(valid, jnp.exp(scores - global_max), 0.0)
        denominator = lax.psum(jnp.sum(weights, axis=-1, keepdims=True), "sq")
        numerator = lax.psum(jnp.einsum("bnt,btd->bnd", weights.astype(jnp.bfloat16), val_new, preferred_element_type=jnp.float32), "sq")
        attended = (numerator / denominator).astype(jnp.bfloat16).reshape(batch, heads_local * head_dim)
        part_sum = jnp.dot(attended, w_out, preferred_element_type=jnp.float32)
        projected = lax.psum(part_sum, "tp")
        out_hidden = (hidden.astype(jnp.float32) + projected + b_out).astype(jnp.bfloat16)
        return out_hidden, key_new, val_new

    cache_spec = P("dp", "sq", None)
    row_spec = P("dp", None)
    in_specs = (row_spec, P("dp"), cache_spec, cache_spec, P(None), P(None), P(None, "tp"), P("tp"), P(None, None), P(None), P("tp", None), P(None))
    out_specs = (row_spec, cache_spec, cache_spec)
    return jax.shard_map(local_step, mesh=mesh, in_specs=in_specs, out_specs=out_specs, check_vma=False)
```

profile of v0, /device:TPU:1, one launch (start us, length us, event | category | flops | bytes accessed | tf_op | source)
XLA Modules:
  0.0 390.6 jit_solution(3861177754152857584)
XLA Ops:
  7.2 0.0 copy-start
  7.2 0.0 copy-start.5
  7.2 0.0 copy-start.6
  7.2 0.0 copy-start.8
  7.2 0.0 all-reduce.3.cloned.1.call-start
  7.3 0.0 copy-start.2
  7.3 2.5 convert_reduce_fusion
  9.8 3.0 fusion.2
  12.9 0.0 copy-done
  12.9 0.0 copy-done.5
  12.9 0.0 copy-done.6
  12.9 0.0 copy-done.8
  12.9 0.0 copy-done.2
  12.9 0.0 copy-start.7
  12.9 1.3 fusion.19
  14.3 0.0 copy-done.7
  14.3 0.0 copy-start.4
  14.3 9.1 %fusion.11 = bf16[256,1536]{1,0:T(8,128)(2,1)S(1)} fusion(bf16[6144,1536]{1,0:T(8,128)(2,1)} %param.18, f32[1536]{0:T(1024)S(1)} %copy-done.7, bf16[256,6144]{1,0:T(8,128)(2,1)S(1)} %copy-done.2, f32[6144]{0:T(1024)S(1)} %copy-done.5, f32[6144]{0:T(1024)S(1)} %copy-done.6, f32[256]{0:T(256)S(1)} %add_rsqrt_fusion, f32[256]{0:T(256)S(1)} %broadcast_multiply_fusion), kind=kOutput, calls=%fused_computation.19 | convolution fusion | flops 4842061824 | bytes 22863872 | tf_op jit(solution)/shard_map/dot_general | solution.py:21
  23.5 0.3 copy.15
  23.8 1.0 copy.16
  24.8 0.0 copy-done.4
  24.8 0.1 broadcast_compare_fusion.1
  25.0 23.3 %broadcast_select_fusion.1 = (bf16[256,256,128]{2,1,0:T(8,128)(2,1)}, bf16[256,256,128]{2,1,0:T(8,128)(2,1)}) fusion(bf16[256,256,128]{2,1,0:T(8,128)(2,1)} %param.14, pred[256,256]{1,0:T(8,128)(4,1)S(1)} %get-tuple-element.8, bf16[256,128]{1,0:T(8,128)(2,1)S(1)} %get-tuple-element.3, bf16[256,256,128]{2,1,0:T(8,128)(2,1)} %param.15, ...), kind=kLoop, calls=%fused_computation.1 | loop fusion | flops 16777216 | bytes 67305472 | tf_op jit(solution)/shard_map/jit(_where)/select_n | solution.py:27
  48.2 12.2 %fusion.8 = (f32[256,12]{1,0:T(8,128)S(1)}, f32[256,12,256]{2,1,0:T(8,128)}) fusion(pred[256,256]{1,0:T(8,128)(4,1)S(1)} %get-tuple-element.7, bf16[256,12,128]{2,1,0:T(8,128)(2,1)S(1)} %copy.16, bf16[256,256,128]{2,1,0:T(8,128)(2,1)} %get-tuple-element.5), kind=kOutput, calls=%fused_computation.15 | convolution fusion | flops 203682816 | bytes 20787200 | tf_op jit(solution)/shard_map/bnd,btd->bnt/dot_general | solution.py:29
  60.4 12.7 %pmax.7 = f32[256,12]{1,0:T(8,128)S(1)} all-reduce(f32[256,12]{1,0:T(8,128)S(1)} %get-tuple-element.9), channel_id=1, replica_groups=mesh['dp'=2,'tp'=4,'sq'=4] {'sq'}, use_global_device_ids=true, to_apply=%region_3.4 | all-reduce | flops 3072 | bytes 24576 | tf_op jit(solution)/shard_map/pmax | solution.py:33
  73.1 11.2 %fusion.12 = f32[256,12,128]{2,1,0:T(8,128)} fusion(bf16[256,256,128]{2,1,0:T(8,128)(2,1)} %get-tuple-element.6, f32[256,12,256]{2,1,0:T(8,128)} %get-tuple-element.10, f32[256,12]{1,0:T(8,128)S(1)} %pmax.7, pred[256,256]{1,0:T(8,128)(4,1)S(1)} %get-tuple-element.7), kind=kOutput, calls=%fused_computation.20 | convolution fusion | flops 205258752 | bytes 21573632 | tf_op jit(solution)/shard_map/bnt,btd->bnd/dot_general | solution.py:36
  84.3 0.0 all-reduce.3.cloned.1.call-update
  84.4 0.0 all-reduce.5.cloned.1.call-start
  84.4 3.7 fusion.9
  88.2 14.6 %psum.22 = f32[256,12]{1,0:T(8,128)S(1)} all-reduce(f32[256,12]{1,0:T(8,128)S(1)} %fusion.9), channel_id=1, replica_groups=mesh['dp'=2,'tp'=4,'sq'=4] {'sq'}, use_global_device_ids=true, to_apply=%region_6.7 | all-reduce | flops 3072 | bytes 24576 | tf_op jit(solution)/shard_map/psum | solution.py:35
  102.8 36.3 %all-reduce.3.cloned.1.call-done = f32[256,12,128]{2,1,0:T(8,128)} async-done(((f32[256,12,128]{2,1,0:T(8,128)}), f32[256,12,128]{2,1,0:T(8,128)}) %all-reduce.3.cloned.1.call-update) | async-done | bytes 1572880 | tf_op jit(solution)/shard_map/psum | solution.py:36
  139.1 1.9 divide_convert_fusion
  141.1 0.9 copy.17
  141.9 13.5 %fusion.26 = f32[256,6144]{1,0:T(8,128)} fusion(bf16[256,1536]{0,1:T(8,128)(2,1)S(1)} %bitcast.9, bf16[1536,6144]{1,0:T(8,128)(2,1)} %param.22), kind=kOutput, calls=%fused_computation.38 | convolution fusion | flops 4831838208 | bytes 25952256 | tf_op jit(solution)/shard_map/dot_general | solution.py:38
  155.4 0.0 copy-start.3
  155.4 0.0 all-reduce.5.cloned.1.call-update
  155.5 0.0 copy-start.1
  155.5 222.0 %all-reduce.5.cloned.1.call-done = f32[256,6144]{1,0:T(8,128)} async-done(((f32[256,6144]{1,0:T(8,128)}), f32[256,6144]{1,0:T(8,128)}) %all-reduce.5.cloned.1.call-update) | async-done | bytes 6291472 | tf_op jit(solution)/shard_map/psum | solution.py:39
  377.4 0.0 copy-done.3
  377.4 6.3 %fusion.7 = bf16[256,6144]{1,0:T(8,128)(2,1)} fusion(f32[256,6144]{1,0:T(8,128)} %all-reduce.5.cloned.1.call-done, bf16[256,6144]{1,0:T(8,128)(2,1)} %param.12, f32[6144]{0:T(1024)S(1)} %copy-done.3), kind=kLoop, calls=%fused_computation.12 | loop fusion | flops 6291456 | bytes 12607488 | tf_op jit(solution)/shard_map/convert_element_type | solution.py:40
  383.7 0.0 copy-done.1
  (4 shorter events, 0.0 us)
Async XLA Ops:
  7.2 5.7 %copy-start = (bf16[6144,256]{1,0:T(8,128)(2,1)S(1)}, bf16[6144,256]{1,0:T(8,128)(2,1)}, u32[]{:S(2)}) copy-start(bf16[6144,256]{1,0:T(8,128)(2,1)} %param.20) | copy-start | bytes 9437188
  7.2 5.7 %copy-start.5 = (f32[6144]{0:T(1024)S(1)}, f32[6144]{0:T(1024)}, u32[]{:S(2)}) copy-start(f32[6144]{0:T(1024)} %param.17) | copy-start | bytes 73732
  7.2 5.7 %copy-start.6 = (f32[6144]{0:T(1024)S(1)}, f32[6144]{0:T(1024)}, u32[]{:S(2)}) copy-start(f32[6144]{0:T(1024)} %param.16) | copy-start | bytes 73732
  7.2 5.7 %copy-start.8 = (f32[256]{0:T(256)S(1)}, f32[256]{0:T(256)}, u32[]{:S(2)}) copy-start(f32[256]{0:T(256)} %param.21) | copy-start | bytes 3076
  7.2 131.9 %all-reduce.3.cloned.1.call-start = ((), (), s32[]{:S(2)}) async-start(), calls=%async_computation | async-start | bytes 4194304 | tf_op jit(solution)/shard_map/psum | solution.py:36
  7.3 5.7 %copy-start.2 = (bf16[256,6144]{1,0:T(8,128)(2,1)S(1)}, bf16[256,6144]{1,0:T(8,128)(2,1)}, u32[]{:S(2)}) copy-start(bf16[256,6144]{1,0:T(8,128)(2,1)} %param.12) | copy-start | bytes 9437188
  12.9 1.4 copy-start.7
  14.3 10.5 %copy-start.4 = (s32[256]{0:T(256)S(1)}, s32[256]{0:T(256)}, u32[]{:S(2)}) copy-start(s32[256]{0:T(256)} %param.13) | copy-start | bytes 3076
  84.4 293.1 %all-reduce.5.cloned.1.call-start = ((), (), s32[]{:S(2)}) async-start(), calls=%async_computation.1 | async-start | bytes 12582912 | tf_op jit(solution)/shard_map/psum | solution.py:39
  155.4 222.0 %copy-start.3 = (f32[6144]{0:T(1024)S(1)}, f32[6144]{0:T(1024)}, u32[]{:S(2)}) copy-start(f32[6144]{0:T(1024)} %param.23) | copy-start | bytes 73732
  155.5 228.3 %copy-start.1 = (bf16[6144,256]{1,0:T(8,128)(2,1)S(1)}, bf16[6144,256]{1,0:T(8,128)(2,1)}, u32[]{:S(2)}) copy-start(bf16[6144,256]{1,0:T(8,128)(2,1)} %param.20) | copy-start | bytes 9437188
Sparse Core Ops, SparseCore 0:
  84.5 54.5 all-reduce.2
  155.6 221.7 all-reduce.4
where the time goes:
time: 392 us; the launch traced here: 391 us
  waiting for transfers between devices  258 us (66%)
  matrix products  47.3 us (12%)
  other arithmetic  41 us (10%)
  blocking collectives  27.3 us (7%)
  between operations  14.3 us (4%)
    psum x1, waiting for transfers between devices, local_step(): projected = lax.psum(part_sum, 'tp')  222 us
    psum x1, waiting for transfers between devices, local_step(): lax.psum(jnp.einsum('bnt,btd->bnd', weights.astype(jnp.bfloat16), val_new...  36.3 us
    select_n x1, other arithmetic, local_step(): key_new = jnp.where(at_slot, key_val[:, None, :head_dim], k_cache)  23.3 us
    psum x1, blocking collectives, local_step(): denominator = lax.psum(jnp.sum(weights, axis=-1, keepdims=True), 'sq')  14.6 us
    dot_general x1, matrix products, local_step(): part_sum = jnp.dot(attended, w_out, preferred_element_type=jnp.float32)  13.5 us
    pmax x1, blocking collectives, local_step(): global_max = lax.pmax(local_max, 'sq')  12.7 us
    dot_general x1, matrix products, local_step(): jnp.einsum('bnd,btd->bnt', query, key_new, preferred_element_type=jnp.flo...  12.2 us
    dot_general x1, matrix products, local_step(): jnp.einsum('bnt,btd->bnd', weights.astype(jnp.bfloat16), val_new, preferr...  11.2 us
  transfers between devices with their start and end apart: 2, of which 2 were waited for; matrix products, arithmetic and copies ran while one was open for 1% of the time, Pallas kernels for 0%

commit v1 on v0

v1 whole, which is shorter than its diff:
```python
import functools

import jax
import jax.numpy as jnp
from jax import lax
from jax.experimental import pallas as pl
from jax.experimental.pallas import tpu as pltpu
from jax.sharding import PartitionSpec as P

MESH = pl.DeviceIdType.MESH
NEG = -1e30
HD = 128
WCOLS = 256
WSLOTS = 3
SEQS = 16
KSLOTS = 6
AHEAD = 3
UNROLL = 16
CHUNKS = 12


def attend_kernel(first_ref, lens_ref, x_hbm, gain_ref, bias_ref, wq_hbm, bq_ref, wkv_hbm, bkv_ref, k_hbm, v_hbm,
                  o_ref, kn_hbm, vn_hbm,
                  x_buf, h_buf, w_buf, q_buf, kv_buf, k_buf, v_buf, s_buf, x_sem, w_sem, kin, vin, kout, vout):
    batch, width = x_buf.shape
    pos = k_hbm.shape[1]
    heads = wq_hbm.shape[1] // HD
    n_q = wq_hbm.shape[1] // WCOLS
    steps = batch // SEQS
    scale = HD ** -0.5

    def w_copy(n, slot):
        cols = pl.ds(pl.multiple_of(n * WCOLS, WCOLS), WCOLS)
        return pltpu.make_async_copy(wq_hbm.at[:, cols], w_buf.at[slot], w_sem.at[slot])

    def cache_in(i):
        slot = lax.rem(i, KSLOTS)
        rows = pl.ds(i * SEQS, SEQS)
        return (pltpu.make_async_copy(k_hbm.at[rows], k_buf.at[slot], kin.at[slot]),
                pltpu.make_async_copy(v_hbm.at[rows], v_buf.at[slot], vin.at[slot]))

    def cache_out(i):
        slot = lax.rem(i, KSLOTS)
        rows = pl.ds(i * SEQS, SEQS)
        return (pltpu.make_async_copy(k_buf.at[slot], kn_hbm.at[rows], kout.at[slot]),
                pltpu.make_async_copy(v_buf.at[slot], vn_hbm.at[rows], vout.at[slot]))

    x_copy = pltpu.make_async_copy(x_hbm, x_buf, x_sem)
    x_copy.start()
    kv_copy = pltpu.make_async_copy(wkv_hbm, w_buf.at[0], w_sem.at[0])
    kv_copy.start()
    for n in range(WSLOTS - 1):
        w_copy(n, n + 1).start()
    for i in range(AHEAD):
        for c in cache_in(i):
            c.start()
    x_copy.wait()

    @pl.loop(0, batch // 16)
    def _(r):
        rows = pl.ds(pl.multiple_of(r * 16, 16), 16)
        wide = x_buf[rows, :].astype(jnp.float32)
        centered = wide - jnp.mean(wide, axis=-1, keepdims=True)
        variance = jnp.mean(centered * centered, axis=-1, keepdims=True)
        normed = centered * lax.rsqrt(variance + 1e-5)
        h_buf[rows, :] = (normed * gain_ref[...] + bias_ref[...]).astype(jnp.bfloat16)

    kv_copy.wait()
    kv = jnp.dot(h_buf[...], w_buf[0], preferred_element_type=jnp.float32) + bkv_ref[...]
    kv_buf[...] = kv.astype(jnp.bfloat16).astype(jnp.float32)

    @pl.loop(0, n_q)
    def _(n):
        slot = lax.rem(n + 1, WSLOTS)

        @pl.when(n + WSLOTS - 1 < n_q)
        def _():
            w_copy(n + WSLOTS - 1, lax.rem(n + WSLOTS, WSLOTS)).start()

        w_copy(n, slot).wait()
        cols = pl.ds(pl.multiple_of(n * WCOLS, WCOLS), WCOLS)
        q = jnp.dot(h_buf[...], w_buf[slot], preferred_element_type=jnp.float32) + bq_ref[:, cols]
        q = q.astype(jnp.bfloat16).astype(jnp.float32)
        for j in range(WCOLS // HD):
            row = pl.multiple_of((n * (WCOLS // HD) + j) * batch, batch)
            q_buf[pl.ds(row, batch), :] = q[:, j * HD:(j + 1) * HD]

    first = first_ref[0]
    lane_pos = first + lax.broadcasted_iota(jnp.int32, (heads, pos), 1)
    head = lax.broadcasted_iota(jnp.int32, (heads, HD), 0)
    lane = lax.broadcasted_iota(jnp.int32, (heads, HD), 1)
    at_top, at_total = lane == head, lane == head + HD // 2
    slab_row = lax.broadcasted_iota(jnp.int32, (16, HD), 0)

    @pl.loop(0, steps)
    def _(i):
        slot = lax.rem(i, KSLOTS)
        for c in cache_in(i):
            c.wait()

        @pl.loop(0, SEQS)
        def _(j):
            b = i * SEQS + j
            at = lens_ref[b] - first
            start = pl.multiple_of((jnp.clip(at, 0, pos - 1) // 16) * 16, 16)
            here = slab_row + start == at
            fresh = kv_buf[pl.ds(b, 1), :]
            for buf, lo in ((k_buf, 0), (v_buf, HD)):
                old = buf[slot, j, pl.ds(start, 16), :].astype(jnp.float32)
                buf[slot, j, pl.ds(start, 16), :] = jnp.where(here, fresh[:, lo:lo + HD], old).astype(jnp.bfloat16)

        @pl.when(i + AHEAD < steps)
        def _():
            @pl.when(i + AHEAD >= KSLOTS)
            def _():
                for c in cache_out(i + AHEAD - KSLOTS):
                    c.wait()
            for c in cache_in(i + AHEAD):
                c.start()

        @pl.loop(0, SEQS // UNROLL)
        def _(g):
            for u in range(UNROLL):
                j = g * UNROLL + u
                q = q_buf[pl.ds(i * SEQS + j, heads, stride=batch), :].astype(jnp.bfloat16)
                s_buf[j] = lax.dot_general(q, k_buf[slot, j], (((1,), (1,)), ((), ())),
                                           preferred_element_type=jnp.float32)

        @pl.loop(0, SEQS // UNROLL)
        def _(g):
            outs = []
            for u in range(UNROLL):
                j = g * UNROLL + u
                b = i * SEQS + j
                valid = lane_pos <= lens_ref[b]
                s = jnp.where(valid, s_buf[j] * scale, NEG)
                top = jnp.max(s, axis=-1, keepdims=True)
                p = jnp.where(valid, jnp.exp(s - top), 0.0)
                total = jnp.sum(p, axis=-1, keepdims=True)
                o = jnp.dot(p.astype(jnp.bfloat16), v_buf[slot, j], preferred_element_type=jnp.float32)
                both = jnp.where(at_top, top, jnp.where(at_total, total, 0.0))
                outs.append((b, o, jnp.sum(both, axis=0, keepdims=True)))
            for b, o, both in outs:
                o_ref[pl.ds(b, heads, stride=batch), :] = o
                o_ref[pl.ds(heads * batch + b, 1), :] = both

        for c in cache_out(i):
            c.start()

    for i in range(max(0, steps - KSLOTS), steps):
        for c in cache_out(i):
            c.wait()


def attend(first, lens, x, gain, bias, wq, bq, wkv, bkv, k_cache, v_cache):
    batch, width = x.shape
    heads = wq.shape[1] // HD
    pos = k_cache.shape[1]
    vmem = pl.BlockSpec(memory_space=pltpu.VMEM)
    smem = pl.BlockSpec(memory_space=pltpu.SMEM)
    hbm = pl.BlockSpec(memory_space=pl.ANY)
    flops = 2 * batch * width * (wq.shape[1] + 2 * HD) + 4 * batch * heads * pos * HD
    return pl.pallas_call(
        attend_kernel,
        out_shape=(jax.ShapeDtypeStruct(((heads + 1) * batch, HD), jnp.float32),
                   jax.ShapeDtypeStruct(k_cache.shape, k_cache.dtype),
                   jax.ShapeDtypeStruct(v_cache.shape, v_cache.dtype)),
        in_specs=[smem, smem, hbm, vmem, vmem, hbm, vmem, hbm, vmem, hbm, hbm],
        out_specs=(vmem, hbm, hbm),
        scratch_shapes=[
            pltpu.VMEM((batch, width), jnp.bfloat16),
            pltpu.VMEM((batch, width), jnp.bfloat16),
            pltpu.VMEM((WSLOTS, width, WCOLS), jnp.bfloat16),
            pltpu.VMEM((heads * batch, HD), jnp.float32),
            pltpu.VMEM((batch, 2 * HD), jnp.float32),
            pltpu.VMEM((KSLOTS, SEQS, pos, HD), jnp.bfloat16),
            pltpu.VMEM((KSLOTS, SEQS, pos, HD), jnp.bfloat16),
            pltpu.VMEM((SEQS, heads, pos), jnp.float32),
            pltpu.SemaphoreType.DMA(()),
            pltpu.SemaphoreType.DMA((WSLOTS,)),
            pltpu.SemaphoreType.DMA((KSLOTS,)),
            pltpu.SemaphoreType.DMA((KSLOTS,)),
            pltpu.SemaphoreType.DMA((KSLOTS,)),
            pltpu.SemaphoreType.DMA((KSLOTS,)),
        ],
        compiler_params=pltpu.CompilerParams(vmem_limit_bytes=56 << 20),
        cost_estimate=pl.CostEstimate(flops=flops, bytes_accessed=100 << 20, transcendentals=batch * heads * pos),
        name="attend",
    )(first, lens, x, gain, bias, wq, bq, wkv, bkv, k_cache, v_cache)


def combine_kernel(part_hbm, w_hbm, x_hbm, b_ref, y_ref,
                   w_buf, x_buf, local, near, mixed, far, a_buf, p_buf, right, left, g_buf,
                   w_sem, in_sem, near_s, near_r, far_s, far_r,
                   rr_s, rr_r, rl_s, rl_r, gr_s, gr_r, gl_s, gl_r, y_s, y_r, d_s, d_r):
    z, s = lax.axis_index("tp"), lax.axis_index("sq")
    y, c = s // 2, lax.rem(s, 2)
    n_z = 4
    heads = part_hbm.shape[0] - 1
    chunks, _, rows, w = p_buf.shape
    own_cols = chunks * w
    core = {"sq": 2 * y + 1 - c}
    across = {"sq": 2 * (1 - y) + c}
    up, down = {"tp": jnp.minimum(z + 1, n_z - 1)}, {"tp": jnp.maximum(z - 1, 0)}

    def remote(src, dst, ss, rs, dev):
        return pltpu.make_async_remote_copy(src, dst, ss, rs, device_id=dev, device_id_type=MESH)

    w_copy = pltpu.make_async_copy(w_hbm, w_buf, w_sem)
    w_copy.start()
    x_cols = pl.ds(pl.multiple_of(z * own_cols, HD), own_cols)
    x_copy = pltpu.make_async_copy(x_hbm.at[pl.ds(pl.multiple_of(s * rows, 16), rows), x_cols], x_buf, in_sem.at[2])
    x_copy.start()
    barrier = pltpu.get_barrier_semaphore()
    for dev in (core, across):
        pl.semaphore_signal(barrier, inc=1, device_id=dev, device_id_type=MESH)

    @pl.when(z < n_z - 1)
    def _():
        pl.semaphore_signal(barrier, inc=1, device_id=up, device_id_type=MESH)

    @pl.when(z > 0)
    def _():
        pl.semaphore_signal(barrier, inc=1, device_id=down, device_id_type=MESH)

    pl.semaphore_wait(barrier, jnp.where((z > 0) & (z < n_z - 1), 4, 3))

    def quarter(q):
        return part_hbm.at[:, pl.ds(pl.multiple_of(q * rows, 8), rows), :]

    def near_copy(k):
        yy = (1 - y) if k == 0 else y
        return remote(quarter(2 * yy + 1 - c), near.at[k], near_s.at[k], near_r.at[k], core)

    def local_copy(k):
        yy = (1 - y) if k == 0 else y
        return pltpu.make_async_copy(quarter(2 * yy + c), local.at[k], in_sem.at[k])

    for k in range(2):
        near_copy(k).start()
        local_copy(k).start()

    def merge(one, two, out):
        ml1, ml2 = one[heads], two[heads]
        top1, top2 = ml1[:, :HD // 2], ml2[:, :HD // 2]
        top = jnp.maximum(top1, top2)
        e1, e2 = jnp.exp(top1 - top), jnp.exp(top2 - top)
        total = e1 * ml1[:, HD // 2:] + e2 * ml2[:, HD // 2:]
        for n in range(heads):
            out[n] = (one[n] * jnp.broadcast_to(e1[:, n:n + 1], (rows, HD))
                      + two[n] * jnp.broadcast_to(e2[:, n:n + 1], (rows, HD)))
        out[heads] = jnp.concatenate([top, total], axis=1)

    local_copy(0).wait()
    near_copy(0).wait_recv()
    merge(local.at[0], near.at[0], mixed)
    far_copy = remote(mixed, far, far_s, far_r, across)
    far_copy.start()
    local_copy(1).wait()
    near_copy(1).wait_recv()
    merge(local.at[1], near.at[1], local.at[0])
    far_copy.wait_recv()
    ml1, ml2 = local[0, heads], far[heads]
    top1, top2 = ml1[:, :HD // 2], ml2[:, :HD // 2]
    top = jnp.maximum(top1, top2)
    e1, e2 = jnp.exp(top1 - top), jnp.exp(top2 - top)
    total = e1 * ml1[:, HD // 2:] + e2 * ml2[:, HD // 2:]
    for n in range(heads):
        num = (local[0, n] * jnp.broadcast_to(e1[:, n:n + 1], (rows, HD))
               + far[n] * jnp.broadcast_to(e2[:, n:n + 1], (rows, HD)))
        a_buf[:, n * HD:(n + 1) * HD] = (num / jnp.broadcast_to(total[:, n:n + 1], (rows, HD))).astype(jnp.bfloat16)
    w_copy.wait()
    x_copy.wait()

    def right_send(j, k):
        return remote(p_buf.at[j, pl.ds(k + 1, n_z - 1 - k)], right.at[j, pl.ds(k + 1, n_z - 1 - k)],
                      rr_s.at[j], rr_r.at[j], up)

    def left_send(j, k):
        return remote(p_buf.at[j, pl.ds(0, k)], left.at[j, pl.ds(0, k)], rl_s.at[j], rl_r.at[j], down)

    def gather_right(j, src, h):
        return remote(g_buf.at[j, s, src], g_buf.at[j, s, src], gr_s.at[j, h], gr_r.at[j, h], up)

    def gather_left(j, src, h):
        return remote(g_buf.at[j, s, src], g_buf.at[j, s, src], gl_s.at[j, h], gl_r.at[j, h], down)

    def across_copy(j):
        return remote(g_buf.at[j, s], g_buf.at[j, s], y_s.at[j], y_r.at[j], across)

    def core_copy(j, k):
        q = s if k == 0 else 2 * (1 - y) + c
        return remote(g_buf.at[j, q], g_buf.at[j, q], d_s.at[j, k], d_r.at[j, k], core)

    def project(j):
        for d in range(n_z):
            cols = pl.ds(pl.multiple_of(d * own_cols + j * w, HD), w)
            p_buf[j, d] = jnp.dot(a_buf[...], w_buf[:, cols], preferred_element_type=jnp.float32)

        @pl.when(z == 0)
        def _():
            right_send(j, 0).start()

        @pl.when(z == n_z - 1)
        def _():
            left_send(j, n_z - 1).start()

    def reduce_hop(j, k):
        @pl.when(z == k)
        def _():
            right_send(j, k - 1).wait_recv()
            for d in range(k + 1, n_z):
                p_buf[j, d] = p_buf[j, d] + right[j, d]
            if k < n_z - 1:
                right_send(j, k).start()

        m = n_z - 1 - k

        @pl.when(z == m)
        def _():
            left_send(j, m + 1).wait_recv()
            for d in range(m):
                p_buf[j, d] = p_buf[j, d] + left[j, d]
            if m > 0:
                left_send(j, m).start()

    def own_block(j):
        cols = pl.ds(pl.multiple_of(j * w, HD), w)
        acc = p_buf[j, z]
        acc = acc + jnp.where(z > 0, right[j, z], 0.0)
        acc = acc + jnp.where(z < n_z - 1, left[j, z], 0.0)
        bias = b_ref[:, pl.ds(pl.multiple_of(z * own_cols + j * w, HD), w)]
        acc = x_buf[:, cols].astype(jnp.float32) + acc + bias
        g_buf[j, s, z] = acc.astype(jnp.bfloat16).astype(jnp.float32)

        @pl.when(z < n_z - 1)
        def _():
            gather_right(j, z, 0).start()

        @pl.when(z > 0)
        def _():
            gather_left(j, z, 0).start()

    def gather_hop(j, h):
        @pl.when(z - 1 - h >= 0)
        def _():
            gather_right(j, z - 1 - h, h).wait_recv()
            if h < n_z - 2:
                @pl.when(z < n_z - 1)
                def _():
                    gather_right(j, z - 1 - h, h + 1).start()

        @pl.when(z + 1 + h <= n_z - 1)
        def _():
            gather_left(j, z + 1 + h, h).wait_recv()
            if h < n_z - 2:
                @pl.when(z > 0)
                def _():
                    gather_left(j, z + 1 + h, h + 1).start()

    def share(j):
        across_copy(j).start()
        core_copy(j, 0).start()

    def take_across(j):
        across_copy_in = remote(g_buf.at[j, 2 * (1 - y) + c], g_buf.at[j, 2 * (1 - y) + c], y_s.at[j], y_r.at[j], across)
        across_copy_in.wait_recv()
        core_copy(j, 1).start()

    def finish(j):
        for k in range(2):
            q = 2 * (y if k == 0 else 1 - y) + 1 - c
            remote(g_buf.at[j, q], g_buf.at[j, q], d_s.at[j, k], d_r.at[j, k], core).wait_recv()
        for q in range(4):
            for d in range(n_z):
                cols = pl.ds(pl.multiple_of(d * own_cols + j * w, HD), w)
                y_ref[q * rows:(q + 1) * rows, cols] = g_buf[j, q, d].astype(jnp.bfloat16)

    def sent(j):
        for k in range(n_z - 1):
            @pl.when(z == k)
            def _():
                right_send(j, k).wait_send()

            @pl.when(z == k + 1)
            def _():
                left_send(j, k + 1).wait_send()

        for h in range(n_z - 1):
            @pl.when((z < n_z - 1) & (z - h >= 0))
            def _():
                gather_right(j, jnp.maximum(z - h, 0), h).wait_send()

            @pl.when((z > 0) & (z + h <= n_z - 1))
            def _():
                gather_left(j, jnp.minimum(z + h, n_z - 1), h).wait_send()
        across_copy(j).wait_send()
        for k in range(2):
            core_copy(j, k).wait_send()

    stages = [project]
    stages += [functools.partial(reduce_hop, k=k) for k in range(1, n_z)]
    stages[-1] = lambda j: (reduce_hop(j, n_z - 1), own_block(j))
    stages += [functools.partial(gather_hop, h=h) for h in range(n_z - 2)]
    stages += [lambda j: (gather_hop(j, n_z - 2), share(j)), take_across, finish, sent]

    @pl.loop(0, chunks + len(stages) - 1)
    def _(t):
        for k in range(len(stages) - 1, -1, -1):
            @pl.when((t >= k) & (t < chunks + k))
            def _():
                stages[k](t - k)

    for k in range(2):
        near_copy(k).wait_send()
    far_copy.wait_send()


def combine(part, w_out, x, b_out):
    planes, batch, _ = part.shape
    heads = planes - 1
    width = x.shape[1]
    rows, n_z = batch // 4, 4
    w = width // n_z // CHUNKS
    vmem = pl.BlockSpec(memory_space=pltpu.VMEM)
    hbm = pl.BlockSpec(memory_space=pl.ANY)
    f32, bf16 = jnp.float32, jnp.bfloat16
    dma = pltpu.SemaphoreType.DMA
    return pl.pallas_call(
        combine_kernel,
        out_shape=jax.ShapeDtypeStruct((batch, width), bf16),
        in_specs=[hbm, hbm, hbm, vmem],
        out_specs=vmem,
        scratch_shapes=[
            pltpu.VMEM(w_out.shape, bf16),
            pltpu.VMEM((rows, width // n_z), bf16),
            pltpu.VMEM((2, planes, rows, HD), f32),
            pltpu.VMEM((2, planes, rows, HD), f32),
            pltpu.VMEM((planes, rows, HD), f32),
            pltpu.VMEM((planes, rows, HD), f32),
            pltpu.VMEM((rows, heads * HD), bf16),
            pltpu.VMEM((CHUNKS, n_z, rows, w), f32),
            pltpu.VMEM((CHUNKS, n_z, rows, w), f32),
            pltpu.VMEM((CHUNKS, n_z, rows, w), f32),
            pltpu.VMEM((CHUNKS, 4, n_z, rows, w), f32),
            dma(()), dma((3,)), dma((2,)), dma((2,)), dma(()), dma(()),
            dma((CHUNKS,)), dma((CHUNKS,)), dma((CHUNKS,)), dma((CHUNKS,)),
            dma((CHUNKS, 3)), dma((CHUNKS, 3)), dma((CHUNKS, 3)), dma((CHUNKS, 3)),
            dma((CHUNKS,)), dma((CHUNKS,)), dma((CHUNKS, 2)), dma((CHUNKS, 2)),
        ],
        compiler_params=pltpu.CompilerParams(vmem_limit_bytes=58 << 20, collective_id=0, has_side_effects=True),
        cost_estimate=pl.CostEstimate(flops=2 * rows * heads * HD * width, bytes_accessed=30 << 20, transcendentals=0),
        name="combine",
    )(part, w_out, x, b_out)


def solution(mesh):
    def local_step(hidden, cache_lens, k_cache, v_cache, ln_gain, ln_bias, w_query, b_query, w_kv, b_kv, w_out, b_out):
        batch, pos_local, head_dim = k_cache.shape
        heads = w_query.shape[1] // head_dim
        first = (lax.axis_index("sq") * pos_local).astype(jnp.int32).reshape(1)
        part, key_new, val_new = attend(first, cache_lens, hidden, ln_gain[None], ln_bias[None], w_query, b_query[None],
                                        w_kv, b_kv[None], k_cache, v_cache)
        out_hidden = combine(part.reshape(heads + 1, batch, head_dim), w_out, hidden, b_out[None])
        return out_hidden, key_new, val_new

    cache_spec = P("dp", "sq", None)
    row_spec = P("dp", None)
    in_specs = (row_spec, P("dp"), cache_spec, cache_spec, P(None), P(None), P(None, "tp"), P("tp"), P(None, None), P(None), P("tp", None), P(None))
    out_specs = (row_spec, cache_spec, cache_spec)
    return jax.shard_map(local_step, mesh=mesh, in_specs=in_specs, out_specs=out_specs, check_vma=False)
```

time: 392 us -> 150 us (0.38)
  waiting for transfers between devices: 258 us -> 0 us
  Pallas kernels: 0 us -> 144 us
  matrix products: 47.3 us -> 0 us
  other arithmetic: 41 us -> 0 us
  blocking collectives: 27.3 us -> 0 us
  between operations: 14.3 us -> 0.65 us
    psum x2 -> x0, waiting for transfers between devices: 258 us -> none  [the longest x1 222 us: local_step(): projected = lax.psum(part_sum, 'tp')]
    pallas_call x0 -> x2, Pallas kernels: none -> 144 us  [the longest x1 103 us: combine(): pl.pallas_call(combine_kernel, out_shape=jax.ShapeDtypeStruct((batch, wid...]
    dot_general x5 -> x0, matrix products: 47.3 us -> none  [the longest x1 13.5 us: local_step(): part_sum = jnp.dot(attended, w_out, preferred_element_type=jnp.float32)]
    select_n x1 -> x0, other arithmetic: 23.3 us -> none  [local_step(): key_new = jnp.where(at_slot, key_val[:, None, :head_dim], k_cache)]
    psum x1 -> x0, blocking collectives: 14.6 us -> none  [local_step(): denominator = lax.psum(jnp.sum(weights, axis=-1, keepdims=True), 'sq')]
    pmax x1 -> x0, blocking collectives: 12.7 us -> none  [local_step(): global_max = lax.pmax(local_max, 'sq')]
    reduce_sum x3 -> x0, other arithmetic: 9.31 us -> none  [the longest x1 3.73 us: local_step(): denominator = lax.psum(jnp.sum(weights, axis=-1, keepdims=True), 'sq')]
    convert_element_type x2 -> x0, other arithmetic: 8.22 us -> none  [the longest x1 6.28 us: local_step(): (hidden.astype(jnp.float32) + projected + b_out).astype(jnp.bfloat16)]
  transfers between devices with their start and end apart: 2 -> 0, of which waited for: 2 -> 0; matrix products, arithmetic and copies ran while one was open for 1% -> 0% of each run, Pallas kernels for 0% -> 0%
where the time goes in v1:
time: 150 us
  Pallas kernels  144 us (96%)
  local copies, waits for them, and re-layouts  5.17 us (3%)
    pallas_call x1, Pallas kernels, combine(): pl.pallas_call(combine_kernel, out_shape=jax.ShapeDtypeStruct((batch, wid...  103 us
    pallas_call x1, Pallas kernels, attend(): pl.pallas_call(attend_kernel, out_shape=(jax.ShapeDtypeStruct(((heads + 1...  41.2 us
    unnamed x1, local copies, waits for them, and re-layouts  3.88 us

profile of v1, /device:TPU:1, one launch (start us, length us, event | category | flops | bytes accessed | tf_op | source)
XLA Modules:
  0.0 149.6 jit_solution(11018735236081921693)
XLA Ops:
  0.6 1.3 broadcast_in_dim.17.bq_ref
  1.9 41.2 %attend.1 = (f32[3328,128]{1,0:T(8,128)}, bf16[256,256,128]{2,1,0:T(8,128)(2,1)}, bf16[256,256,128]{2,1,0:T(8,128)(2,1)}) custom-call(s32[1]{0:T(128)} %bitcast.first_ref, s32[256]{0:T(256)} %lens_ref.1, bf16[256,6144]{1,0:T(8,128)(2,1)} %x_hbm.3, f32[1,6144]{1,0:T(1,128)} %bitcast.7, f32[1,6144]{1,0:T(1,128)} %bitcast.8, bf16[6144,1536]{1,0:T(8,128)(2,1)} %wq_hbm.1, ...), custom_call_target="tpu_custom_call" | custom-call | flops 6039797760 | bytes 104857600 | tf_op jit(solution)/shard_map/attend/pallas_call | solution.py:163
  43.2 102.5 %combine.1 = bf16[256,6144]{1,0:T(8,128)(2,1)} custom-call(f32[13,256,128]{2,1,0:T(8,128)} %bitcast.6, bf16[1536,6144]{1,0:T(8,128)(2,1)} %w_hbm.1, bf16[256,6144]{1,0:T(8,128)(2,1)} %x_hbm.3, f32[1,6144]{1,0:T(1,128)} %bitcast.9), custom_call_target="tpu_custom_call" | custom-call | flops 1207959552 | bytes 31457280 | tf_op jit(solution)/shard_map/combine/pallas_call | solution.py:429
  145.7 3.9 %copy.16 = bf16[256,6144]{1,0:T(8,128)(2,1)} copy(bf16[256,6144]{1,0:T(8,128)(2,1)} %combine.1) | data formatting | bytes 6291456

commit v2 on v1

v2 whole, which is shorter than its diff:
```python
import functools

import jax
import jax.numpy as jnp
from jax import lax
from jax.experimental import pallas as pl
from jax.experimental.pallas import tpu as pltpu
from jax.sharding import PartitionSpec as P

MESH = pl.DeviceIdType.MESH
NEG = -1e30
HD = 128
WCOLS = 256
WSLOTS = 3
SEQS = 16
KSLOTS = 6
AHEAD = 3
UNROLL = 16
CHUNKS = 4
NCOLS = 1536


def attend_kernel(first_ref, lens_ref, x_hbm, gain_ref, bias_ref, wq_hbm, bq_ref, wkv_hbm, bkv_ref, k_hbm, v_hbm,
                  o_ref, kn_hbm, vn_hbm,
                  x_buf, h_buf, w_buf, q_buf, kv_buf, k_buf, v_buf, s_buf, x_sem, w_sem, kin, vin, kout, vout):
    batch, width = x_buf.shape
    pos = k_hbm.shape[1]
    heads = wq_hbm.shape[1] // HD
    n_q = wq_hbm.shape[1] // WCOLS
    steps = batch // SEQS
    scale = HD ** -0.5

    def w_copy(n, slot):
        cols = pl.ds(pl.multiple_of(n * WCOLS, WCOLS), WCOLS)
        return pltpu.make_async_copy(wq_hbm.at[:, cols], w_buf.at[slot], w_sem.at[slot])

    def cache_in(i):
        slot = lax.rem(i, KSLOTS)
        rows = pl.ds(i * SEQS, SEQS)
        return (pltpu.make_async_copy(k_hbm.at[rows], k_buf.at[slot], kin.at[slot]),
                pltpu.make_async_copy(v_hbm.at[rows], v_buf.at[slot], vin.at[slot]))

    def cache_out(i):
        slot = lax.rem(i, KSLOTS)
        rows = pl.ds(i * SEQS, SEQS)
        return (pltpu.make_async_copy(k_buf.at[slot], kn_hbm.at[rows], kout.at[slot]),
                pltpu.make_async_copy(v_buf.at[slot], vn_hbm.at[rows], vout.at[slot]))

    x_copy = pltpu.make_async_copy(x_hbm, x_buf, x_sem)
    x_copy.start()
    kv_copy = pltpu.make_async_copy(wkv_hbm, w_buf.at[0], w_sem.at[0])
    kv_copy.start()
    for n in range(WSLOTS - 1):
        w_copy(n, n + 1).start()
    for i in range(AHEAD):
        for c in cache_in(i):
            c.start()
    x_copy.wait()

    @pl.loop(0, batch // 16)
    def _(r):
        rows = pl.ds(pl.multiple_of(r * 16, 16), 16)
        wide = x_buf[rows, :].astype(jnp.float32)
        centered = wide - jnp.mean(wide, axis=-1, keepdims=True)
        variance = jnp.mean(centered * centered, axis=-1, keepdims=True)
        normed = centered * lax.rsqrt(variance + 1e-5)
        h_buf[rows, :] = (normed * gain_ref[...] + bias_ref[...]).astype(jnp.bfloat16)

    kv_copy.wait()
    kv = jnp.dot(h_buf[...], w_buf[0], preferred_element_type=jnp.float32) + bkv_ref[...]
    kv_buf[...] = kv.astype(jnp.bfloat16).astype(jnp.float32)

    @pl.loop(0, n_q)
    def _(n):
        slot = lax.rem(n + 1, WSLOTS)

        @pl.when(n + WSLOTS - 1 < n_q)
        def _():
            w_copy(n + WSLOTS - 1, lax.rem(n + WSLOTS, WSLOTS)).start()

        w_copy(n, slot).wait()
        cols = pl.ds(pl.multiple_of(n * WCOLS, WCOLS), WCOLS)
        q = jnp.dot(h_buf[...], w_buf[slot], preferred_element_type=jnp.float32) + bq_ref[:, cols]
        q = q.astype(jnp.bfloat16).astype(jnp.float32)
        for j in range(WCOLS // HD):
            row = pl.multiple_of((n * (WCOLS // HD) + j) * batch, batch)
            q_buf[pl.ds(row, batch), :] = q[:, j * HD:(j + 1) * HD]

    first = first_ref[0]
    lane_pos = first + lax.broadcasted_iota(jnp.int32, (heads, pos), 1)
    head = lax.broadcasted_iota(jnp.int32, (heads, HD), 0)
    lane = lax.broadcasted_iota(jnp.int32, (heads, HD), 1)
    at_top, at_total = lane == head, lane == head + HD // 2
    slab_row = lax.broadcasted_iota(jnp.int32, (16, HD), 0)

    @pl.loop(0, steps)
    def _(i):
        slot = lax.rem(i, KSLOTS)
        for c in cache_in(i):
            c.wait()

        @pl.loop(0, SEQS)
        def _(j):
            b = i * SEQS + j
            at = lens_ref[b] - first
            start = pl.multiple_of((jnp.clip(at, 0, pos - 1) // 16) * 16, 16)
            here = slab_row + start == at
            fresh = kv_buf[pl.ds(b, 1), :]
            for buf, lo in ((k_buf, 0), (v_buf, HD)):
                old = buf[slot, j, pl.ds(start, 16), :].astype(jnp.float32)
                buf[slot, j, pl.ds(start, 16), :] = jnp.where(here, fresh[:, lo:lo + HD], old).astype(jnp.bfloat16)

        @pl.when(i + AHEAD < steps)
        def _():
            @pl.when(i + AHEAD >= KSLOTS)
            def _():
                for c in cache_out(i + AHEAD - KSLOTS):
                    c.wait()
            for c in cache_in(i + AHEAD):
                c.start()

        @pl.loop(0, SEQS // UNROLL)
        def _(g):
            for u in range(UNROLL):
                j = g * UNROLL + u
                q = q_buf[pl.ds(i * SEQS + j, heads, stride=batch), :].astype(jnp.bfloat16)
                s_buf[j] = lax.dot_general(q, k_buf[slot, j], (((1,), (1,)), ((), ())),
                                           preferred_element_type=jnp.float32)

        @pl.loop(0, SEQS // UNROLL)
        def _(g):
            outs = []
            for u in range(UNROLL):
                j = g * UNROLL + u
                b = i * SEQS + j
                valid = lane_pos <= lens_ref[b]
                s = jnp.where(valid, s_buf[j] * scale, NEG)
                top = jnp.max(s, axis=-1, keepdims=True)
                p = jnp.where(valid, jnp.exp(s - top), 0.0)
                total = jnp.sum(p, axis=-1, keepdims=True)
                o = jnp.dot(p.astype(jnp.bfloat16), v_buf[slot, j], preferred_element_type=jnp.float32)
                both = jnp.where(at_top, top, jnp.where(at_total, total, 0.0))
                outs.append((b, o, jnp.sum(both, axis=0, keepdims=True)))
            for b, o, both in outs:
                o_ref[pl.ds(b, heads, stride=batch), :] = o
                o_ref[pl.ds(heads * batch + b, 1), :] = both

        for c in cache_out(i):
            c.start()

    for i in range(max(0, steps - KSLOTS), steps):
        for c in cache_out(i):
            c.wait()


def attend(first, lens, x, gain, bias, wq, bq, wkv, bkv, k_cache, v_cache):
    batch, width = x.shape
    heads = wq.shape[1] // HD
    pos = k_cache.shape[1]
    vmem = pl.BlockSpec(memory_space=pltpu.VMEM)
    smem = pl.BlockSpec(memory_space=pltpu.SMEM)
    hbm = pl.BlockSpec(memory_space=pl.ANY)
    flops = 2 * batch * width * (wq.shape[1] + 2 * HD) + 4 * batch * heads * pos * HD
    return pl.pallas_call(
        attend_kernel,
        out_shape=(jax.ShapeDtypeStruct(((heads + 1) * batch, HD), jnp.float32),
                   jax.ShapeDtypeStruct(k_cache.shape, k_cache.dtype),
                   jax.ShapeDtypeStruct(v_cache.shape, v_cache.dtype)),
        in_specs=[smem, smem, hbm, vmem, vmem, hbm, vmem, hbm, vmem, hbm, hbm],
        out_specs=(vmem, hbm, hbm),
        scratch_shapes=[
            pltpu.VMEM((batch, width), jnp.bfloat16),
            pltpu.VMEM((batch, width), jnp.bfloat16),
            pltpu.VMEM((WSLOTS, width, WCOLS), jnp.bfloat16),
            pltpu.VMEM((heads * batch, HD), jnp.float32),
            pltpu.VMEM((batch, 2 * HD), jnp.float32),
            pltpu.VMEM((KSLOTS, SEQS, pos, HD), jnp.bfloat16),
            pltpu.VMEM((KSLOTS, SEQS, pos, HD), jnp.bfloat16),
            pltpu.VMEM((SEQS, heads, pos), jnp.float32),
            pltpu.SemaphoreType.DMA(()),
            pltpu.SemaphoreType.DMA((WSLOTS,)),
            pltpu.SemaphoreType.DMA((KSLOTS,)),
            pltpu.SemaphoreType.DMA((KSLOTS,)),
            pltpu.SemaphoreType.DMA((KSLOTS,)),
            pltpu.SemaphoreType.DMA((KSLOTS,)),
        ],
        compiler_params=pltpu.CompilerParams(vmem_limit_bytes=56 << 20),
        cost_estimate=pl.CostEstimate(flops=flops, bytes_accessed=100 << 20, transcendentals=batch * heads * pos),
        name="attend",
    )(first, lens, x, gain, bias, wq, bq, wkv, bkv, k_cache, v_cache)


def signal_peers(barrier, z, n_z, core, across):
    for dev in (core, across):
        pl.semaphore_signal(barrier, inc=1, device_id=dev, device_id_type=MESH)

    @pl.when(z < n_z - 1)
    def _():
        pl.semaphore_signal(barrier, inc=1, device_id={"tp": jnp.minimum(z + 1, n_z - 1)}, device_id_type=MESH)

    @pl.when(z > 0)
    def _():
        pl.semaphore_signal(barrier, inc=1, device_id={"tp": jnp.maximum(z - 1, 0)}, device_id_type=MESH)

    pl.semaphore_wait(barrier, jnp.where((z > 0) & (z < n_z - 1), 4, 3))


def remote(src, dst, ss, rs, dev):
    return pltpu.make_async_remote_copy(src, dst, ss, rs, device_id=dev, device_id_type=MESH)


def exchange_stages(part, w_buf, x_buf, b_ref, y_ref, near, mixed, far, a_buf, p_buf, in_a, in_b, g_buf,
                    near_s, near_r, far_s, far_r, line_s, line_r, y_s, y_r, d_s, d_r):
    z, s = lax.axis_index("tp"), lax.axis_index("sq")
    y, c = s // 2, lax.rem(s, 2)
    heads = part.shape[0] - 1
    chunks, _, rc, half = p_buf.shape
    rows = chunks * rc
    core = {"sq": 2 * y + 1 - c}
    across = {"sq": 2 * (1 - y) + c}
    up, down = {"tp": jnp.minimum(z + 1, 3)}, {"tp": jnp.maximum(z - 1, 0)}
    place = (z, 3 - z)
    nxt, prv = (up, down), (down, up)

    def quarter(q, t):
        return part.at[:, pl.ds(pl.multiple_of(q * rows + t * rc, 8), rc), :]

    def near_copy(t, k):
        yy = (1 - y) if k == 0 else y
        return remote(quarter(2 * yy + 1 - c, t), near.at[t, k], near_s.at[t, k], near_r.at[t, k], core)

    def far_copy(t):
        return remote(mixed.at[t], far.at[t], far_s.at[t], far_r.at[t], across)

    def weights(ml1, ml2):
        top1, top2 = ml1[:, :HD // 2], ml2[:, :HD // 2]
        top = jnp.maximum(top1, top2)
        e1, e2 = jnp.exp(top1 - top), jnp.exp(top2 - top)
        return top, e1, e2, e1 * ml1[:, HD // 2:] + e2 * ml2[:, HD // 2:]

    def wide(v, n):
        return jnp.broadcast_to(v[:, n:n + 1], (rc, HD))

    def merge(one, two, out):
        top, e1, e2, total = weights(one[heads], two[heads])
        for n in range(heads):
            out[n] = one[n] * wide(e1, n) + two[n] * wide(e2, n)
        out[heads] = jnp.concatenate([top, total], axis=1)

    def give(t):
        for k in range(2):
            near_copy(t, k).start()

    def meet(t):
        near_copy(t, 0).wait_recv()
        merge(quarter(2 * (1 - y) + c, t), near.at[t, 0], mixed.at[t])
        far_copy(t).start()
        near_copy(t, 1).wait_recv()
        merge(quarter(s, t), near.at[t, 1], near.at[t, 1])

    def line(kind, t, f):
        src = p_buf.at[t, f] if kind < 3 else g_buf.at[t, s, f]
        dst = (in_a.at[t, f], in_a.at[t, f], in_b.at[t, f])[kind] if kind < 3 else g_buf.at[t, s, f]
        to = (nxt, prv, prv, prv, nxt, nxt)[kind][f]
        send, recv = (0, 0, 0, 0, 1, 1)[kind], (0, 0, 1, 0, 1, 0)[kind]
        return remote(src, dst, line_s.at[t, f, send], line_r.at[t, f, recv], to)

    def project(t):
        far_copy(t).wait_recv()
        one, two = near.at[t, 1], far.at[t]
        top, e1, e2, total = weights(one[heads], two[heads])
        for n in range(heads):
            num = one[n] * wide(e1, n) + two[n] * wide(e2, n)
            a_buf[:, n * HD:(n + 1) * HD] = (num / wide(total, n)).astype(jnp.bfloat16)
        for f in range(2):
            @pl.loop(0, half // NCOLS)
            def _(m):
                cols = pl.ds(pl.multiple_of(f * half + m * NCOLS, NCOLS), NCOLS)
                p_buf[t, f, :, pl.ds(pl.multiple_of(m * NCOLS, NCOLS), NCOLS)] = jnp.dot(
                    a_buf[...], w_buf[:, cols], preferred_element_type=jnp.float32)

            for p, kind in ((0, 0), (3, 1)):
                @pl.when(place[f] == p)
                def _():
                    line(kind, t, f).start()

    def add_first(t):
        for f in range(2):
            @pl.when(place[f] == 2)
            def _():
                line(1, t, f).wait_recv()
                p_buf[t, f] = p_buf[t, f] + in_a[t, f]
                line(2, t, f).start()

    def spread(t, f):
        remote(g_buf.at[t, s, f], g_buf.at[t, s, f], y_s.at[t, f], y_r.at[t, f], across).start()
        remote(g_buf.at[t, s, f], g_buf.at[t, s, f], d_s.at[t, 0, f], d_r.at[t, 0, f], core).start()

    def add_last(t):
        for f in range(2):
            @pl.when(place[f] == 1)
            def _():
                line(0, t, f).wait_recv()
                line(2, t, f).wait_recv()
                mine = x_buf[pl.ds(pl.multiple_of(t * rc, 8), rc), f * half:(f + 1) * half]
                acc = mine + (p_buf[t, f] + in_a[t, f] + in_b[t, f]) + b_ref[:, f * half:(f + 1) * half]
                g_buf[t, s, f] = acc.astype(jnp.bfloat16).astype(jnp.float32)
                line(3, t, f).start()
                line(4, t, f).start()
                spread(t, f)

    def pass_on(t):
        for f in range(2):
            @pl.when(place[f] == 2)
            def _():
                line(4, t, f).wait_recv()
                line(5, t, f).start()
                spread(t, f)

            @pl.when(place[f] == 0)
            def _():
                line(3, t, f).wait_recv()
                spread(t, f)

    def reach_end(t):
        for f in range(2):
            @pl.when(place[f] == 3)
            def _():
                line(5, t, f).wait_recv()
                spread(t, f)

    other = 2 * (1 - y) + c

    def take_across(t):
        for f in range(2):
            block = g_buf.at[t, other, f]
            remote(block, block, y_s.at[t, f], y_r.at[t, f], across).wait_recv()
            remote(block, block, d_s.at[t, 1, f], d_r.at[t, 1, f], core).start()

    def finish(t):
        for k in range(2):
            q = 2 * (y if k == 0 else 1 - y) + 1 - c
            for f in range(2):
                block = g_buf.at[t, q, f]
                remote(block, block, d_s.at[t, k, f], d_r.at[t, k, f], core).wait_recv()
        per = 16 // rc

        @pl.when(lax.rem(t, per) == per - 1)
        def _():
            t0 = t - (per - 1)
            for q in range(4):
                for f in range(2):
                    block = jnp.concatenate([g_buf[t0 + i, q, f] for i in range(per)], axis=0)
                    y_ref[pl.ds(pl.multiple_of(q * rows + t0 * rc, 16), 16), f * half:(f + 1) * half] = block.astype(
                        jnp.bfloat16)

    def sent(t):
        for k in range(2):
            near_copy(t, k).wait_send()
        far_copy(t).wait_send()
        for f in range(2):
            for p, kinds in ((0, (0,)), (1, (3, 4)), (2, (2, 5)), (3, (1,))):
                @pl.when(place[f] == p)
                def _():
                    for kind in kinds:
                        line(kind, t, f).wait_send()
            block = g_buf.at[t, s, f]
            remote(block, block, y_s.at[t, f], y_r.at[t, f], across).wait_send()
            for k, q in ((0, s), (1, other)):
                block = g_buf.at[t, q, f]
                remote(block, block, d_s.at[t, k, f], d_r.at[t, k, f], core).wait_send()

    return [give, meet, project, add_first, add_last, pass_on, reach_end, take_across, finish, sent]


def run_stages(stages, chunks):
    @pl.loop(0, chunks + len(stages) - 1)
    def _(t):
        for k in range(len(stages) - 1, -1, -1):
            @pl.when((t >= k) & (t < chunks + k))
            def _():
                stages[k](t - k)


def exchange_scratch(planes, rows, width):
    f32, bf16, dma, rc, half = jnp.float32, jnp.bfloat16, pltpu.SemaphoreType.DMA, rows // CHUNKS, width // 2
    n = CHUNKS
    return [
        pltpu.VMEM((n, 2, planes, rc, HD), f32), pltpu.VMEM((n, planes, rc, HD), f32), pltpu.VMEM((n, planes, rc, HD), f32),
        pltpu.VMEM((rc, (planes - 1) * HD), bf16),
        pltpu.VMEM((n, 2, rc, half), f32), pltpu.VMEM((n, 2, rc, half), f32), pltpu.VMEM((n, 2, rc, half), f32),
        pltpu.VMEM((n, 4, 2, rc, half), f32),
        dma((n, 2)), dma((n, 2)), dma((n,)), dma((n,)), dma((n, 2, 2)), dma((n, 2, 2)),
        dma((n, 2)), dma((n, 2)), dma((n, 2, 2)), dma((n, 2, 2)),
    ]


def combine_kernel(part_hbm, w_hbm, x_hbm, b_ref, y_ref, part, w_buf, x_bf, x_buf, w_sem, in_sem, *rest):
    z, s = lax.axis_index("tp"), lax.axis_index("sq")
    y, c = s // 2, lax.rem(s, 2)
    rows = x_buf.shape[0]
    w_copy = pltpu.make_async_copy(w_hbm, w_buf, w_sem)
    w_copy.start()
    x_copy = pltpu.make_async_copy(x_hbm.at[pl.ds(pl.multiple_of(s * rows, 16), rows)], x_bf, in_sem.at[0])
    x_copy.start()
    p_copy = pltpu.make_async_copy(part_hbm, part, in_sem.at[1])
    p_copy.start()
    signal_peers(pltpu.get_barrier_semaphore(), z, 4, {"sq": 2 * y + 1 - c}, {"sq": 2 * (1 - y) + c})
    p_copy.wait()
    x_copy.wait()
    x_buf[...] = x_bf[...].astype(jnp.float32)
    w_copy.wait()
    run_stages(exchange_stages(part, w_buf, x_buf, b_ref, y_ref, *rest), CHUNKS)


def combine(part, w_out, x, b_out):
    planes, batch, _ = part.shape
    width = x.shape[1]
    rows = batch // 4
    vmem = pl.BlockSpec(memory_space=pltpu.VMEM)
    hbm = pl.BlockSpec(memory_space=pl.ANY)
    f32, bf16 = jnp.float32, jnp.bfloat16
    dma = pltpu.SemaphoreType.DMA
    return pl.pallas_call(
        combine_kernel,
        out_shape=jax.ShapeDtypeStruct((batch, width), bf16),
        in_specs=[hbm, hbm, hbm, vmem],
        out_specs=vmem,
        scratch_shapes=[
            pltpu.VMEM(part.shape, f32),
            pltpu.VMEM(w_out.shape, bf16),
            pltpu.VMEM((rows, width), bf16),
            pltpu.VMEM((rows, width), f32),
            dma(()), dma((2,))] + exchange_scratch(planes, rows, width),
        compiler_params=pltpu.CompilerParams(vmem_limit_bytes=58 << 20, collective_id=0, has_side_effects=True),
        cost_estimate=pl.CostEstimate(flops=2 * rows * w_out.size, bytes_accessed=30 << 20, transcendentals=0),
        name="combine",
    )(part, w_out, x, b_out)


def solution(mesh):
    def local_step(hidden, cache_lens, k_cache, v_cache, ln_gain, ln_bias, w_query, b_query, w_kv, b_kv, w_out, b_out):
        batch, pos_local, head_dim = k_cache.shape
        heads = w_query.shape[1] // head_dim
        first = (lax.axis_index("sq") * pos_local).astype(jnp.int32).reshape(1)
        part, key_new, val_new = attend(first, cache_lens, hidden, ln_gain[None], ln_bias[None], w_query, b_query[None],
                                        w_kv, b_kv[None], k_cache, v_cache)
        out_hidden = combine(part.reshape(heads + 1, batch, head_dim), w_out, hidden, b_out[None])
        return out_hidden, key_new, val_new

    cache_spec = P("dp", "sq", None)
    row_spec = P("dp", None)
    in_specs = (row_spec, P("dp"), cache_spec, cache_spec, P(None), P(None), P(None, "tp"), P("tp"), P(None, None), P(None), P("tp", None), P(None))
    out_specs = (row_spec, cache_spec, cache_spec)
    return jax.shard_map(local_step, mesh=mesh, in_specs=in_specs, out_specs=out_specs, check_vma=False)
```

time: 150 us -> 127 us (0.85)
  Pallas kernels: 144 us -> 120 us
    pallas_call x1, Pallas kernels: 103 us -> 79.3 us  [combine(): pl.pallas_call(combine_kernel, out_shape=jax.ShapeDtypeStruct((batch, wid...]
where the time goes in v2:
time: 127 us; the launch traced here: 126 us
  Pallas kernels  120 us (94%)
  local copies, waits for them, and re-layouts  5.17 us (4%)
    pallas_call x1, Pallas kernels, combine(): pl.pallas_call(combine_kernel, out_shape=jax.ShapeDtypeStruct((batch, wid...  79.3 us
    pallas_call x1, Pallas kernels, attend(): pl.pallas_call(attend_kernel, out_shape=(jax.ShapeDtypeStruct(((heads + 1...  41.2 us
    unnamed x1, local copies, waits for them, and re-layouts  3.88 us

profile of v2, /device:TPU:1, one launch (start us, length us, event | category | flops | bytes accessed | tf_op | source)
XLA Modules:
  0.0 126.3 jit_solution(7168989420836539918)
XLA Ops:
  0.6 1.3 %broadcast_in_dim.17.bq_ref = f32[1,1536]{1,0:T(1,128)} reshape(f32[1536]{0:T(1024)} %param.19) | data formatting | bytes 12288 | tf_op jit(solution)/shard_map/broadcast_in_dim | solution.py:446
  1.9 41.2 %attend.1 = (f32[3328,128]{1,0:T(8,128)}, bf16[256,256,128]{2,1,0:T(8,128)(2,1)}, bf16[256,256,128]{2,1,0:T(8,128)(2,1)}) custom-call(s32[1]{0:T(128)} %bitcast.first_ref, s32[256]{0:T(256)} %lens_ref.1, bf16[256,6144]{1,0:T(8,128)(2,1)} %x_hbm.3, f32[1,6144]{1,0:T(1,128)} %bitcast.7, f32[1,6144]{1,0:T(1,128)} %bitcast.8, bf16[6144,1536]{1,0:T(8,128)(2,1)} %wq_hbm.1, ...), custom_call_target="tpu_custom_call" | custom-call | flops 6039797760 | bytes 104857600 | tf_op jit(solution)/shard_map/attend/pallas_call | solution.py:164
  43.2 79.3 %combine.1 = bf16[256,6144]{1,0:T(8,128)(2,1)} custom-call(f32[13,256,128]{2,1,0:T(8,128)} %bitcast.6, bf16[1536,6144]{1,0:T(8,128)(2,1)} %w_hbm.1, bf16[256,6144]{1,0:T(8,128)(2,1)} %x_hbm.3, f32[1,6144]{1,0:T(1,128)} %bitcast.9), custom_call_target="tpu_custom_call" | custom-call | flops 1207959552 | bytes 31457280 | tf_op jit(solution)/shard_map/combine/pallas_call | solution.py:424
  122.4 3.9 %copy.16 = bf16[256,6144]{1,0:T(8,128)(2,1)} copy(bf16[256,6144]{1,0:T(8,128)(2,1)} %combine.1) | data formatting | bytes 6291456

commit v3 on v2

v3 whole, which is shorter than its diff:
```python
import functools

import jax
import jax.numpy as jnp
from jax import lax
from jax.experimental import pallas as pl
from jax.experimental.pallas import tpu as pltpu
from jax.sharding import PartitionSpec as P

MESH = pl.DeviceIdType.MESH
NEG = -1e30
HD = 128
WCOLS = 256
WSLOTS = 3
SEQS = 16
FIRST = 4
PER_STEP = 2
UNROLL = 16
PATCH = 8
CHUNKS = 4
DEPTH = 2
SPLIT = 4


def attend_kernel(first_ref, lens_ref, x_hbm, gain_ref, bias_ref, wq_hbm, bq_ref, wkv_hbm, bkv_ref, k_hbm, v_hbm,
                  o_ref, kn_hbm, vn_hbm,
                  x_buf, h_buf, w_buf, q_buf, kv_buf, k_buf, v_buf, s_buf, x_sem, w_sem, kin, vin, kout, vout):
    batch, width = x_buf.shape
    pos = k_hbm.shape[1]
    heads = wq_hbm.shape[1] // HD
    n_q = wq_hbm.shape[1] // WCOLS
    steps = batch // SEQS
    scale = HD ** -0.5

    def w_copy(n, slot):
        cols = pl.ds(pl.multiple_of(n * WCOLS, WCOLS), WCOLS)
        return pltpu.make_async_copy(wq_hbm.at[:, cols], w_buf.at[slot], w_sem.at[slot])

    def cache_in(i):
        slot, rows = i, pl.ds(i * SEQS, SEQS)
        return (pltpu.make_async_copy(k_hbm.at[rows], k_buf.at[slot], kin.at[slot]),
                pltpu.make_async_copy(v_hbm.at[rows], v_buf.at[slot], vin.at[slot]))

    def cache_out(i):
        slot, rows = i, pl.ds(i * SEQS, SEQS)
        return (pltpu.make_async_copy(k_buf.at[slot], kn_hbm.at[rows], kout.at[slot]),
                pltpu.make_async_copy(v_buf.at[slot], vn_hbm.at[rows], vout.at[slot]))

    x_copy = pltpu.make_async_copy(x_hbm, x_buf, x_sem)
    x_copy.start()
    kv_copy = pltpu.make_async_copy(wkv_hbm, w_buf.at[0], w_sem.at[0])
    kv_copy.start()
    for n in range(WSLOTS - 1):
        w_copy(n, n + 1).start()
    for i in range(FIRST):
        for c in cache_in(i):
            c.start()
    x_copy.wait()

    @pl.loop(0, batch // 16)
    def _(r):
        rows = pl.ds(pl.multiple_of(r * 16, 16), 16)
        wide = x_buf[rows, :].astype(jnp.float32)
        centered = wide - jnp.mean(wide, axis=-1, keepdims=True)
        variance = jnp.mean(centered * centered, axis=-1, keepdims=True)
        normed = centered * lax.rsqrt(variance + 1e-5)
        h_buf[rows, :] = (normed * gain_ref[...] + bias_ref[...]).astype(jnp.bfloat16)

    kv_copy.wait()
    kv = jnp.dot(h_buf[...], w_buf[0], preferred_element_type=jnp.float32) + bkv_ref[...]
    kv_buf[...] = kv.astype(jnp.bfloat16).astype(jnp.float32)

    @pl.loop(0, n_q)
    def _(n):
        slot = lax.rem(n + 1, WSLOTS)

        @pl.when(n + WSLOTS - 1 < n_q)
        def _():
            w_copy(n + WSLOTS - 1, lax.rem(n + WSLOTS, WSLOTS)).start()

        for i in range(PER_STEP):
            @pl.when(FIRST + n * PER_STEP + i < steps)
            def _():
                for c in cache_in(FIRST + n * PER_STEP + i):
                    c.start()

        w_copy(n, slot).wait()
        cols = pl.ds(pl.multiple_of(n * WCOLS, WCOLS), WCOLS)
        q = jnp.dot(h_buf[...], w_buf[slot], preferred_element_type=jnp.float32) + bq_ref[:, cols]
        q = q.astype(jnp.bfloat16).astype(jnp.float32)
        for j in range(WCOLS // HD):
            row = pl.multiple_of((n * (WCOLS // HD) + j) * batch, batch)
            q_buf[pl.ds(row, batch), :] = q[:, j * HD:(j + 1) * HD]

    first = first_ref[0]
    lane_pos = first + lax.broadcasted_iota(jnp.int32, (heads, pos), 1)
    head = lax.broadcasted_iota(jnp.int32, (heads, HD), 0)
    lane = lax.broadcasted_iota(jnp.int32, (heads, HD), 1)
    at_top, at_total = lane == head, lane == head + HD // 2
    slab_row = lax.broadcasted_iota(jnp.int32, (16, HD), 0)

    @pl.loop(0, steps)
    def _(i):
        slot = i
        for c in cache_in(i):
            c.wait()

        @pl.loop(0, SEQS // PATCH)
        def _(g):
            slabs = []
            for u in range(PATCH):
                j = g * PATCH + u
                b = i * SEQS + j
                at = lens_ref[b] - first
                start = pl.multiple_of((jnp.clip(at, 0, pos - 1) // 16) * 16, 16)
                here = slab_row == at - start
                fresh = kv_buf[pl.ds(b, 1), :]
                for buf, lo in ((k_buf, 0), (v_buf, HD)):
                    old = buf[slot, j, pl.ds(start, 16), :].astype(jnp.float32)
                    new = jnp.where(here, fresh[:, lo:lo + HD], old).astype(jnp.bfloat16)
                    slabs.append((buf, j, start, new))
            for buf, j, start, new in slabs:
                buf[slot, j, pl.ds(start, 16), :] = new

        @pl.loop(0, SEQS // UNROLL)
        def _(g):
            for u in range(UNROLL):
                j = g * UNROLL + u
                q = q_buf[pl.ds(i * SEQS + j, heads, stride=batch), :].astype(jnp.bfloat16)
                s_buf[j] = lax.dot_general(q, k_buf[slot, j], (((1,), (1,)), ((), ())),
                                           preferred_element_type=jnp.float32)

        @pl.loop(0, SEQS // UNROLL)
        def _(g):
            outs = []
            for u in range(UNROLL):
                j = g * UNROLL + u
                b = i * SEQS + j
                valid = lane_pos <= lens_ref[b]
                s = jnp.where(valid, s_buf[j] * scale, NEG)
                top = jnp.max(s, axis=-1, keepdims=True)
                p = jnp.where(valid, jnp.exp(s - top), 0.0)
                total = jnp.sum(p, axis=-1, keepdims=True)
                o = jnp.dot(p.astype(jnp.bfloat16), v_buf[slot, j], preferred_element_type=jnp.float32)
                both = jnp.where(at_top, top, jnp.where(at_total, total, 0.0))
                outs.append((b, o, jnp.sum(both, axis=0, keepdims=True)))
            for b, o, both in outs:
                o_ref[pl.ds(b, heads, stride=batch), :] = o
                o_ref[pl.ds(heads * batch + b, 1), :] = both

        for c in cache_out(i):
            c.start()

    for i in range(steps):
        for c in cache_out(i):
            c.wait()


def attend(first, lens, x, gain, bias, wq, bq, wkv, bkv, k_cache, v_cache):
    batch, width = x.shape
    heads = wq.shape[1] // HD
    pos = k_cache.shape[1]
    vmem = pl.BlockSpec(memory_space=pltpu.VMEM)
    smem = pl.BlockSpec(memory_space=pltpu.SMEM)
    hbm = pl.BlockSpec(memory_space=pl.ANY)
    flops = 2 * batch * width * (wq.shape[1] + 2 * HD) + 4 * batch * heads * pos * HD
    return pl.pallas_call(
        attend_kernel,
        out_shape=(jax.ShapeDtypeStruct(((heads + 1) * batch, HD), jnp.float32),
                   jax.ShapeDtypeStruct(k_cache.shape, k_cache.dtype),
                   jax.ShapeDtypeStruct(v_cache.shape, v_cache.dtype)),
        in_specs=[smem, smem, hbm, vmem, vmem, hbm, vmem, hbm, vmem, hbm, hbm],
        out_specs=(vmem, hbm, hbm),
        scratch_shapes=[
            pltpu.VMEM((batch, width), jnp.bfloat16),
            pltpu.VMEM((batch, width), jnp.bfloat16),
            pltpu.VMEM((WSLOTS, width, WCOLS), jnp.bfloat16),
            pltpu.VMEM((heads * batch, HD), jnp.float32),
            pltpu.VMEM((batch, 2 * HD), jnp.float32),
            pltpu.VMEM((batch // SEQS, SEQS, pos, HD), jnp.bfloat16),
            pltpu.VMEM((batch // SEQS, SEQS, pos, HD), jnp.bfloat16),
            pltpu.VMEM((SEQS, heads, pos), jnp.float32),
            pltpu.SemaphoreType.DMA(()),
            pltpu.SemaphoreType.DMA((WSLOTS,)),
            pltpu.SemaphoreType.DMA((batch // SEQS,)),
            pltpu.SemaphoreType.DMA((batch // SEQS,)),
            pltpu.SemaphoreType.DMA((batch // SEQS,)),
            pltpu.SemaphoreType.DMA((batch // SEQS,)),
        ],
        compiler_params=pltpu.CompilerParams(vmem_limit_bytes=60 << 20),
        cost_estimate=pl.CostEstimate(flops=flops, bytes_accessed=100 << 20, transcendentals=batch * heads * pos),
        name="attend",
    )(first, lens, x, gain, bias, wq, bq, wkv, bkv, k_cache, v_cache)


def signal_peers(barrier, z, n_z, core, across):
    for dev in (core, across):
        pl.semaphore_signal(barrier, inc=1, device_id=dev, device_id_type=MESH)

    @pl.when(z < n_z - 1)
    def _():
        pl.semaphore_signal(barrier, inc=1, device_id={"tp": jnp.minimum(z + 1, n_z - 1)}, device_id_type=MESH)

    @pl.when(z > 0)
    def _():
        pl.semaphore_signal(barrier, inc=1, device_id={"tp": jnp.maximum(z - 1, 0)}, device_id_type=MESH)

    pl.semaphore_wait(barrier, jnp.where((z > 0) & (z < n_z - 1), 4, 3))


def remote(src, dst, ss, rs, dev):
    return pltpu.make_async_remote_copy(src, dst, ss, rs, device_id=dev, device_id_type=MESH)


def combine_kernel(part_hbm, w_hbm, x_hbm, b_ref, y_hbm,
                   part, w_buf, x_buf, y_buf, near, mixed, far, a_buf, p_buf, in_a, in_b, g_buf,
                   w_sem, x_sem, part_sem, out_sem,
                   near_s, near_r, far_s, far_r, line_s, line_r, y_s, y_r, d_s, d_r):
    z, s = lax.axis_index("tp"), lax.axis_index("sq")
    y, c = s // 2, lax.rem(s, 2)
    heads = part.shape[1] - 1
    units, _, rc, piece = p_buf.shape
    half = piece * SPLIT
    chunks = units // SPLIT
    rows = chunks * rc
    other = 2 * (1 - y) + c
    core, across = {"sq": 2 * y + 1 - c}, {"sq": other}
    up, down = {"tp": jnp.minimum(z + 1, 3)}, {"tp": jnp.maximum(z - 1, 0)}
    place = (z, 3 - z)
    nxt, prv = (up, down), (down, up)

    def part_copy(k):
        some = pl.ds(pl.multiple_of((2 * ((1 - y) if k == 0 else y) + c) * rows, 8), rows)
        return pltpu.make_async_copy(part_hbm.at[:, some], part.at[k], part_sem.at[k])

    def near_copy(k):
        some = pl.ds(pl.multiple_of((2 * ((1 - y) if k == 0 else y) + 1 - c) * rows, 8), rows)
        return remote(part_hbm.at[:, some], near.at[k], near_s.at[k], near_r.at[k], core)

    def far_copy(t):
        return remote(mixed.at[t], far.at[t], far_s.at[t], far_r.at[t], across)

    def line(kind, u, f):
        src = p_buf.at[u, f] if kind < 3 else g_buf.at[u, s, f]
        dst = (in_a.at[u, f], in_a.at[u, f], in_b.at[u, f])[kind] if kind < 3 else g_buf.at[u, s, f]
        to = (nxt, prv, prv, prv, nxt, nxt)[kind][f]
        send, recv = (0, 0, 0, 0, 1, 1)[kind], (0, 0, 1, 0, 1, 0)[kind]
        return remote(src, dst, line_s.at[u, f, send], line_r.at[u, f, recv], to)

    def across_copy(u, q, f):
        return remote(g_buf.at[u, q, f], g_buf.at[u, q, f], y_s.at[u, f], y_r.at[u, f], across)

    def core_copy(u, k, q, f):
        return remote(g_buf.at[u, q, f], g_buf.at[u, q, f], d_s.at[u, k, f], d_r.at[u, k, f], core)

    def out_copy(t, q):
        some = pl.ds(pl.multiple_of(q * rows + t * rc, 16), rc)
        return pltpu.make_async_copy(y_buf.at[some], y_hbm.at[some], out_sem.at[t, q])

    for k in range(2):
        part_copy(k).start()
    x_copy = pltpu.make_async_copy(x_hbm.at[pl.ds(pl.multiple_of(s * rows, 16), rows)], x_buf, x_sem)
    x_copy.start()
    signal_peers(pltpu.get_barrier_semaphore(), z, 4, core, across)
    for k in range(2):
        near_copy(k).start()
    w_copy = pltpu.make_async_copy(w_hbm, w_buf, w_sem)
    w_copy.start()

    def weights(ml1, ml2):
        top1, top2 = ml1[:, :HD // 2], ml2[:, :HD // 2]
        top = jnp.maximum(top1, top2)
        e1, e2 = jnp.exp(top1 - top), jnp.exp(top2 - top)
        return top, e1, e2, e1 * ml1[:, HD // 2:] + e2 * ml2[:, HD // 2:]

    def wide(v, n):
        return jnp.broadcast_to(v[:, n:n + 1], (rc, HD))

    def rows_of(t):
        return pl.ds(pl.multiple_of(t * rc, 8), rc)

    def merged(k, t):
        some = rows_of(t)
        top, e1, e2, total = weights(part[k, heads, some, :], near[k, heads, some, :])
        for n in range(heads):
            yield part[k, n, some, :] * wide(e1, n) + near[k, n, some, :] * wide(e2, n)
        yield jnp.concatenate([top, total], axis=1)

    part_copy(0).wait()
    near_copy(0).wait_recv()

    @pl.loop(0, chunks)
    def _(t):
        for n, value in enumerate(merged(0, t)):
            mixed[t, n] = value
        far_copy(t).start()

    part_copy(1).wait()
    near_copy(1).wait_recv()

    @pl.loop(0, chunks)
    def _(t):
        for n, value in enumerate(merged(1, t)):
            part[1, n, rows_of(t), :] = value

    x_copy.wait()
    w_copy.wait()

    def project(u):
        t, h = u // SPLIT, lax.rem(u, SPLIT)

        @pl.when(h == 0)
        def _():
            far_copy(t).wait_recv()
            some = rows_of(t)
            top, e1, e2, total = weights(part[1, heads, some, :], far[t, heads])
            for n in range(heads):
                num = part[1, n, some, :] * wide(e1, n) + far[t, n] * wide(e2, n)
                a_buf[:, n * HD:(n + 1) * HD] = (num / wide(total, n)).astype(jnp.bfloat16)

        for f in range(2):
            cols = pl.ds(pl.multiple_of(f * half + h * piece, HD), piece)
            p_buf[u, f] = jnp.dot(a_buf[...], w_buf[:, cols], preferred_element_type=jnp.float32)
            for p, kind in ((0, 0), (3, 1)):
                @pl.when(place[f] == p)
                def _():
                    line(kind, u, f).start()

    def add_first(u):
        for f in range(2):
            @pl.when(place[f] == 2)
            def _():
                line(1, u, f).wait_recv()
                p_buf[u, f] = p_buf[u, f] + in_a[u, f]
                line(2, u, f).start()

    def spread(u, f):
        across_copy(u, s, f).start()
        core_copy(u, 0, s, f).start()

    def add_last(u):
        t, h = u // SPLIT, lax.rem(u, SPLIT)
        for f in range(2):
            @pl.when(place[f] == 1)
            def _():
                line(0, u, f).wait_recv()
                line(2, u, f).wait_recv()
                cols = pl.ds(pl.multiple_of(f * half + h * piece, HD), piece)
                mine = x_buf[pl.ds(pl.multiple_of(t * rc, 16), rc), cols].astype(jnp.float32)
                acc = mine + (p_buf[u, f] + in_a[u, f] + in_b[u, f]) + b_ref[:, cols]
                g_buf[u, s, f] = acc.astype(jnp.bfloat16).astype(jnp.float32)
                line(4, u, f).start()
                line(3, u, f).start()
                spread(u, f)

    def pass_on(u):
        for f in range(2):
            @pl.when(place[f] == 2)
            def _():
                line(4, u, f).wait_recv()
                line(5, u, f).start()
                spread(u, f)

            @pl.when(place[f] == 0)
            def _():
                line(3, u, f).wait_recv()
                spread(u, f)

    def reach_end(u):
        for f in range(2):
            @pl.when(place[f] == 3)
            def _():
                line(5, u, f).wait_recv()
                spread(u, f)

    def take_across(u):
        for f in range(2):
            across_copy(u, other, f).wait_recv()
            core_copy(u, 1, other, f).start()

    def finish(u):
        t, h = u // SPLIT, lax.rem(u, SPLIT)
        for k in range(2):
            for f in range(2):
                core_copy(u, k, 2 * (y if k == 0 else 1 - y) + 1 - c, f).wait_recv()
        for q in range(4):
            for f in range(2):
                cols = pl.ds(pl.multiple_of(f * half + h * piece, HD), piece)
                y_buf[pl.ds(pl.multiple_of(q * rows + t * rc, 16), rc), cols] = g_buf[u, q, f].astype(jnp.bfloat16)

        @pl.when(h == SPLIT - 1)
        def _():
            for q in range(4):
                out_copy(t, q).start()

    def sent(u):
        for f in range(2):
            for p, kinds in ((0, (0,)), (1, (3, 4)), (2, (2, 5)), (3, (1,))):
                @pl.when(place[f] == p)
                def _():
                    for kind in kinds:
                        line(kind, u, f).wait_send()
            across_copy(u, s, f).wait_send()
            for k, q in ((0, s), (1, other)):
                core_copy(u, k, q, f).wait_send()

    stages = [project, add_first, add_last, pass_on, reach_end, take_across, finish, sent]

    offsets = [DEPTH * k for k in range(len(stages) - 1)]
    offsets.append(offsets[-1] + 1)

    @pl.loop(0, units + offsets[-1])
    def _(it):
        for k in range(len(stages) - 1, -1, -1):
            @pl.when((it >= offsets[k]) & (it < units + offsets[k]))
            def _():
                stages[k](it - offsets[k])

    for k in range(2):
        near_copy(k).wait_send()
    for t in range(chunks):
        far_copy(t).wait_send()
        for q in range(4):
            out_copy(t, q).wait()


def combine(part, w_out, x, b_out):
    planes, batch, _ = part.shape
    width = x.shape[1]
    rows = batch // 4
    rc, piece, units = rows // CHUNKS, width // 2 // SPLIT, CHUNKS * SPLIT
    vmem = pl.BlockSpec(memory_space=pltpu.VMEM)
    hbm = pl.BlockSpec(memory_space=pl.ANY)
    f32, bf16, dma = jnp.float32, jnp.bfloat16, pltpu.SemaphoreType.DMA
    return pl.pallas_call(
        combine_kernel,
        out_shape=jax.ShapeDtypeStruct((batch, width), bf16),
        in_specs=[hbm, hbm, hbm, vmem],
        out_specs=hbm,
        scratch_shapes=[
            pltpu.VMEM((2, planes, rows, HD), f32),
            pltpu.VMEM(w_out.shape, bf16),
            pltpu.VMEM((rows, width), bf16),
            pltpu.VMEM((batch, width), bf16),
            pltpu.VMEM((2, planes, rows, HD), f32),
            pltpu.VMEM((CHUNKS, planes, rc, HD), f32),
            pltpu.VMEM((CHUNKS, planes, rc, HD), f32),
            pltpu.VMEM((rc, (planes - 1) * HD), bf16),
            pltpu.VMEM((units, 2, rc, piece), f32),
            pltpu.VMEM((units, 2, rc, piece), f32),
            pltpu.VMEM((units, 2, rc, piece), f32),
            pltpu.VMEM((units, 4, 2, rc, piece), f32),
            dma(()), dma(()), dma((2,)), dma((CHUNKS, 4)),
            dma((2,)), dma((2,)), dma((CHUNKS,)), dma((CHUNKS,)), dma((units, 2, 2)), dma((units, 2, 2)),
            dma((units, 2)), dma((units, 2)), dma((units, 2, 2)), dma((units, 2, 2)),
        ],
        compiler_params=pltpu.CompilerParams(vmem_limit_bytes=58 << 20, collective_id=0, has_side_effects=True),
        cost_estimate=pl.CostEstimate(flops=2 * rows * w_out.size, bytes_accessed=30 << 20, transcendentals=0),
        name="combine",
    )(part, w_out, x, b_out)


def solution(mesh):
    def local_step(hidden, cache_lens, k_cache, v_cache, ln_gain, ln_bias, w_query, b_query, w_kv, b_kv, w_out, b_out):
        batch, pos_local, head_dim = k_cache.shape
        heads = w_query.shape[1] // head_dim
        first = (lax.axis_index("sq") * pos_local).astype(jnp.int32).reshape(1)
        part, key_new, val_new = attend(first, cache_lens, hidden, ln_gain[None], ln_bias[None], w_query, b_query[None],
                                        w_kv, b_kv[None], k_cache, v_cache)
        out_hidden = combine(part.reshape(heads + 1, batch, head_dim), w_out, hidden, b_out[None])
        return out_hidden, key_new, val_new

    cache_spec = P("dp", "sq", None)
    row_spec = P("dp", None)
    in_specs = (row_spec, P("dp"), cache_spec, cache_spec, P(None), P(None), P(None, "tp"), P("tp"), P(None, None), P(None), P("tp", None), P(None))
    out_specs = (row_spec, cache_spec, cache_spec)
    return jax.shard_map(local_step, mesh=mesh, in_specs=in_specs, out_specs=out_specs, check_vma=False)
```

time: 127 us -> 112 us (0.88)
  Pallas kernels: 120 us -> 105 us
    pallas_call x1, Pallas kernels: 79.3 us -> 66.3 us  [combine(): pl.pallas_call(combine_kernel, out_shape=jax.ShapeDtypeStruct((batch, wid...]
    pallas_call x1, Pallas kernels: 41.2 us -> 39.1 us  [attend(): pl.pallas_call(attend_kernel, out_shape=(jax.ShapeDtypeStruct(((heads + 1...]
where the time goes in v3:
time: 112 us; the launch traced here: 111 us
  Pallas kernels  105 us (94%)
  local copies, waits for them, and re-layouts  5.17 us (5%)
    pallas_call x1, Pallas kernels, combine(): pl.pallas_call(combine_kernel, out_shape=jax.ShapeDtypeStruct((batch, wid...  66.3 us
    pallas_call x1, Pallas kernels, attend(): pl.pallas_call(attend_kernel, out_shape=(jax.ShapeDtypeStruct(((heads + 1...  39.1 us
    unnamed x1, local copies, waits for them, and re-layouts  3.88 us

profile of v3, /device:TPU:1, one launch (start us, length us, event | category | flops | bytes accessed | tf_op | source)
XLA Modules:
  0.0 111.2 jit_solution(12083244179659508046)
XLA Ops:
  0.6 1.3 %broadcast_in_dim.17.bq_ref = f32[1,1536]{1,0:T(1,128)} reshape(f32[1536]{0:T(1024)} %param.19) | data formatting | bytes 12288 | tf_op jit(solution)/shard_map/broadcast_in_dim | solution.py:468
  1.9 39.1 %attend.1 = (f32[3328,128]{1,0:T(8,128)}, bf16[256,256,128]{2,1,0:T(8,128)(2,1)}, bf16[256,256,128]{2,1,0:T(8,128)(2,1)}) custom-call(s32[1]{0:T(128)} %bitcast.first_ref, s32[256]{0:T(256)} %lens_ref.1, bf16[256,6144]{1,0:T(8,128)(2,1)} %x_hbm.3, f32[1,6144]{1,0:T(1,128)} %bitcast.7, f32[1,6144]{1,0:T(1,128)} %bitcast.8, bf16[6144,1536]{1,0:T(8,128)(2,1)} %wq_hbm.1, ...), custom_call_target="tpu_custom_call" | custom-call | flops 6039797760 | bytes 104857600 | tf_op jit(solution)/shard_map/attend/pallas_call | solution.py:167
  41.1 66.3 %combine.1 = bf16[256,6144]{1,0:T(8,128)(2,1)} custom-call(f32[13,256,128]{2,1,0:T(8,128)} %bitcast.6, bf16[1536,6144]{1,0:T(8,128)(2,1)} %w_hbm.1, bf16[256,6144]{1,0:T(8,128)(2,1)} %x_hbm.3, f32[1,6144]{1,0:T(1,128)} %bitcast.9), custom_call_target="tpu_custom_call" | custom-call | flops 1207959552 | bytes 31457280 | tf_op jit(solution)/shard_map/combine/pallas_call | solution.py:435
  107.3 3.9 %copy.16 = bf16[256,6144]{1,0:T(8,128)(2,1)} copy(bf16[256,6144]{1,0:T(8,128)(2,1)} %combine.1) | data formatting | bytes 6291456

commit v4 on v3

--- a/solution.py
+++ b/solution.py
@@ -11,12 +11,12 @@
 NEG = -1e30
 HD = 128
 WCOLS = 256
-WSLOTS = 3
-SEQS = 16
-FIRST = 4
-PER_STEP = 2
-UNROLL = 16
-PATCH = 8
+WSLOTS = 4
+SEQS = 32
+FIRST = 2
+PER_STEP = 1
+UNROLL = 32
+PATCH = 16
 CHUNKS = 4
 DEPTH = 2
 SPLIT = 4
@@ -85,12 +85,11 @@
                     c.start()
 
         w_copy(n, slot).wait()
-        cols = pl.ds(pl.multiple_of(n * WCOLS, WCOLS), WCOLS)
-        q = jnp.dot(h_buf[...], w_buf[slot], preferred_element_type=jnp.float32) + bq_ref[:, cols]
-        q = q.astype(jnp.bfloat16).astype(jnp.float32)
+        q = jnp.dot(h_buf[...], w_buf[slot], preferred_element_type=jnp.float32)
         for j in range(WCOLS // HD):
             row = pl.multiple_of((n * (WCOLS // HD) + j) * batch, batch)
-            q_buf[pl.ds(row, batch), :] = q[:, j * HD:(j + 1) * HD]
+            one = q[:, j * HD:(j + 1) * HD] + bq_ref[pl.ds(n * (WCOLS // HD) + j, 1), :]
+            q_buf[pl.ds(row, batch), :] = one.astype(jnp.bfloat16).astype(jnp.float32)
 
     first = first_ref[0]
     lane_pos = first + lax.broadcasted_iota(jnp.int32, (heads, pos), 1)
@@ -162,7 +161,7 @@
     pos = k_cache.shape[1]
     vmem = pl.BlockSpec(memory_space=pltpu.VMEM)
     smem = pl.BlockSpec(memory_space=pltpu.SMEM)
-    hbm = pl.BlockSpec(memory_space=pl.ANY)
+    hbm = pl.BlockSpec(memory_space=pltpu.HBM)
     flops = 2 * batch * width * (wq.shape[1] + 2 * HD) + 4 * batch * heads * pos * HD
     return pl.pallas_call(
         attend_kernel,
@@ -233,9 +232,12 @@
         some = pl.ds(pl.multiple_of((2 * ((1 - y) if k == 0 else y) + c) * rows, 8), rows)
         return pltpu.make_async_copy(part_hbm.at[:, some], part.at[k], part_sem.at[k])
 
-    def near_copy(k):
-        some = pl.ds(pl.multiple_of((2 * ((1 - y) if k == 0 else y) + 1 - c) * rows, 8), rows)
-        return remote(part_hbm.at[:, some], near.at[k], near_s.at[k], near_r.at[k], core)
+    def rows_of(t):
+        return pl.ds(pl.multiple_of(t * rc, 8), rc)
+
+    def near_copy(k, t):
+        some = pl.ds(pl.multiple_of((2 * ((1 - y) if k == 0 else y) + 1 - c) * rows + t * rc, 8), rc)
+        return remote(part_hbm.at[:, some], near.at[k, :, rows_of(t)], near_s.at[k, t], near_r.at[k, t], core)
 
     def far_copy(t):
         return remote(mixed.at[t], far.at[t], far_s.at[t], far_r.at[t], across)
@@ -263,7 +265,8 @@
     x_copy.start()
     signal_peers(pltpu.get_barrier_semaphore(), z, 4, core, across)
     for k in range(2):
-        near_copy(k).start()
+        for t in range(chunks):
+            near_copy(k, t).start()
     w_copy = pltpu.make_async_copy(w_hbm, w_buf, w_sem)
     w_copy.start()
 
@@ -276,10 +279,8 @@
     def wide(v, n):
         return jnp.broadcast_to(v[:, n:n + 1], (rc, HD))
 
-    def rows_of(t):
-        return pl.ds(pl.multiple_of(t * rc, 8), rc)
-
     def merged(k, t):
+        near_copy(k, t).wait_recv()
         some = rows_of(t)
         top, e1, e2, total = weights(part[k, heads, some, :], near[k, heads, some, :])
         for n in range(heads):
@@ -287,7 +288,6 @@
         yield jnp.concatenate([top, total], axis=1)
 
     part_copy(0).wait()
-    near_copy(0).wait_recv()
 
     @pl.loop(0, chunks)
     def _(t):
@@ -296,7 +296,6 @@
         far_copy(t).start()
 
     part_copy(1).wait()
-    near_copy(1).wait_recv()
 
     @pl.loop(0, chunks)
     def _(t):
@@ -416,9 +415,9 @@
             def _():
                 stages[k](it - offsets[k])
 
-    for k in range(2):
-        near_copy(k).wait_send()
     for t in range(chunks):
+        for k in range(2):
+            near_copy(k, t).wait_send()
         far_copy(t).wait_send()
         for q in range(4):
             out_copy(t, q).wait()
@@ -451,7 +450,7 @@
             pltpu.VMEM((units, 2, rc, piece), f32),
             pltpu.VMEM((units, 4, 2, rc, piece), f32),
             dma(()), dma(()), dma((2,)), dma((CHUNKS, 4)),
-            dma((2,)), dma((2,)), dma((CHUNKS,)), dma((CHUNKS,)), dma((units, 2, 2)), dma((units, 2, 2)),
+            dma((2, CHUNKS)), dma((2, CHUNKS)), dma((CHUNKS,)), dma((CHUNKS,)), dma((units, 2, 2)), dma((units, 2, 2)),
             dma((units, 2)), dma((units, 2)), dma((units, 2, 2)), dma((units, 2, 2)),
         ],
         compiler_params=pltpu.CompilerParams(vmem_limit_bytes=58 << 20, collective_id=0, has_side_effects=True),
@@ -465,7 +464,7 @@
         batch, pos_local, head_dim = k_cache.shape
         heads = w_query.shape[1] // head_dim
         first = (lax.axis_index("sq") * pos_local).astype(jnp.int32).reshape(1)
-        part, key_new, val_new = attend(first, cache_lens, hidden, ln_gain[None], ln_bias[None], w_query, b_query[None],
+        part, key_new, val_new = attend(first, cache_lens, hidden, ln_gain[None], ln_bias[None], w_query, b_query.reshape(-1, HD),
                                         w_kv, b_kv[None], k_cache, v_cache)
         out_hidden = combine(part.reshape(heads + 1, batch, head_dim), w_out, hidden, b_out[None])
         return out_hidden, key_new, val_new

time: 112 us -> 106 us (0.946)
  Pallas kernels: 105 us -> 101 us
  local copies, waits for them, and re-layouts: 5.17 us -> 3.88 us
    pallas_call x1, Pallas kernels: 39.1 us -> 35.3 us  [attend(): pl.pallas_call(attend_kernel, out_shape=(jax.ShapeDtypeStruct(((heads + 1...]
    broadcast_in_dim x1 -> x0, local copies, waits for them, and re-layouts: 1.29 us -> none  [local_step(): b_query[None]]
where the time goes in v4:
time: 106 us
  Pallas kernels  101 us (95%)
  local copies, waits for them, and re-layouts  3.88 us (4%)
    pallas_call x1, Pallas kernels, combine(): pl.pallas_call(combine_kernel, out_shape=jax.ShapeDtypeStruct((batch, wid...  65.9 us
    pallas_call x1, Pallas kernels, attend(): pl.pallas_call(attend_kernel, out_shape=(jax.ShapeDtypeStruct(((heads + 1...  35.3 us
    unnamed x1, local copies, waits for them, and re-layouts  3.88 us

profile of v4, /device:TPU:1, one launch (start us, length us, event | category | flops | bytes accessed | tf_op | source)
XLA Modules:
  0.0 105.7 jit_solution(15929375740484126358)
XLA Ops:
  0.6 35.3 %attend.1 = (f32[3328,128]{1,0:T(8,128)}, bf16[256,256,128]{2,1,0:T(8,128)(2,1)}, bf16[256,256,128]{2,1,0:T(8,128)(2,1)}) custom-call(s32[1]{0:T(128)} %bitcast.first_ref, s32[256]{0:T(256)} %lens_ref.1, bf16[256,6144]{1,0:T(8,128)(2,1)} %x_hbm.3, f32[1,6144]{1,0:T(1,128)} %bitcast.8, f32[1,6144]{1,0:T(1,128)} %bitcast.9, bf16[6144,1536]{1,0:T(8,128)(2,1)} %wq_hbm.1, ...), custom_call_target="tpu_custom_call" | custom-call | flops 6039797760 | bytes 104857600 | tf_op jit(solution)/shard_map/attend/pallas_call | solution.py:166
  36.0 65.9 %combine.1 = bf16[256,6144]{1,0:T(8,128)(2,1)} custom-call(f32[13,256,128]{2,1,0:T(8,128)} %bitcast.7, bf16[1536,6144]{1,0:T(8,128)(2,1)} %w_hbm.1, bf16[256,6144]{1,0:T(8,128)(2,1)} %x_hbm.3, f32[1,6144]{1,0:T(1,128)} %bitcast.10), custom_call_target="tpu_custom_call" | custom-call | flops 1207959552 | bytes 31457280 | tf_op jit(solution)/shard_map/combine/pallas_call | solution.py:434
  101.9 3.9 %copy.16 = bf16[256,6144]{1,0:T(8,128)(2,1)} copy(bf16[256,6144]{1,0:T(8,128)(2,1)} %combine.1) | data formatting | bytes 6291456

commit v5 on v4

--- a/solution.py
+++ b/solution.py
@@ -430,11 +430,12 @@
     rc, piece, units = rows // CHUNKS, width // 2 // SPLIT, CHUNKS * SPLIT
     vmem = pl.BlockSpec(memory_space=pltpu.VMEM)
     hbm = pl.BlockSpec(memory_space=pl.ANY)
+    pinned = pl.BlockSpec(memory_space=pltpu.HBM)
     f32, bf16, dma = jnp.float32, jnp.bfloat16, pltpu.SemaphoreType.DMA
     return pl.pallas_call(
         combine_kernel,
         out_shape=jax.ShapeDtypeStruct((batch, width), bf16),
-        in_specs=[hbm, hbm, hbm, vmem],
+        in_specs=[pinned, pinned, pinned, vmem],
         out_specs=hbm,
         scratch_shapes=[
             pltpu.VMEM((2, planes, rows, HD), f32),
@@ -453,7 +454,7 @@
             dma((2, CHUNKS)), dma((2, CHUNKS)), dma((CHUNKS,)), dma((CHUNKS,)), dma((units, 2, 2)), dma((units, 2, 2)),
             dma((units, 2)), dma((units, 2)), dma((units, 2, 2)), dma((units, 2, 2)),
         ],
-        compiler_params=pltpu.CompilerParams(vmem_limit_bytes=58 << 20, collective_id=0, has_side_effects=True),
+        compiler_params=pltpu.CompilerParams(vmem_limit_bytes=48 << 20, collective_id=0, has_side_effects=True),
         cost_estimate=pl.CostEstimate(flops=2 * rows * w_out.size, bytes_accessed=30 << 20, transcendentals=0),
         name="combine",
     )(part, w_out, x, b_out)

time: 106 us -> 105 us (level)
    unnamed x1 -> x5, local copies, waits for them, and re-layouts: 3.88 us -> 3.12 us
where the time goes in v5:
time: 105 us
  Pallas kernels  101 us (96%)
  local copies, waits for them, and re-layouts  3.12 us (3%)
    pallas_call x1, Pallas kernels, combine(): pl.pallas_call(combine_kernel, out_shape=jax.ShapeDtypeStruct((batch, wid...  65.9 us
    pallas_call x1, Pallas kernels, attend(): pl.pallas_call(attend_kernel, out_shape=(jax.ShapeDtypeStruct(((heads + 1...  35.4 us
    unnamed x5, local copies, waits for them, and re-layouts  3.12 us

profile of v5, /device:TPU:1, one launch (start us, length us, event | category | flops | bytes accessed | tf_op | source)
XLA Modules:
  0.0 105.1 jit_solution(10739108405868716865)
XLA Ops:
  0.6 0.0 copy-start.1
  0.6 35.4 %attend.1 = (f32[3328,128]{1,0:T(8,128)}, bf16[256,256,128]{2,1,0:T(8,128)(2,1)}, bf16[256,256,128]{2,1,0:T(8,128)(2,1)}) custom-call(s32[1]{0:T(128)} %bitcast.first_ref, s32[256]{0:T(256)} %lens_ref.1, bf16[256,6144]{1,0:T(8,128)(2,1)} %x_hbm.3, f32[1,6144]{1,0:T(1,128)} %bitcast.9, f32[1,6144]{1,0:T(1,128)} %bitcast.10, bf16[6144,1536]{1,0:T(8,128)(2,1)} %wq_hbm.1, ...), custom_call_target="tpu_custom_call" | custom-call | flops 6039797760 | bytes 104857600 | tf_op jit(solution)/shard_map/attend/pallas_call | solution.py:166
  36.0 0.0 copy-done.1
  36.0 0.0 copy-start
  36.0 1.4 %copy-done = f32[3328,128]{1,0:T(8,128)S(1)} copy-done((f32[3328,128]{1,0:T(8,128)S(1)}, f32[3328,128]{1,0:T(8,128)}, u32[]{:S(2)}) %copy-start) | copy-done | bytes 1703960
  37.5 65.9 %combine.1 = bf16[256,6144]{1,0:T(8,128)(2,1)S(1)} custom-call(f32[13,256,128]{2,1,0:T(8,128)S(1)} %bitcast.7, bf16[1536,6144]{1,0:T(8,128)(2,1)} %w_hbm.1, bf16[256,6144]{1,0:T(8,128)(2,1)} %x_hbm.3, f32[1,6144]{1,0:T(1,128)S(1)} %bitcast.8), custom_call_target="tpu_custom_call" | custom-call | flops 1207959552 | bytes 31457280 | tf_op jit(solution)/shard_map/combine/pallas_call | solution.py:435
  103.4 1.7 %copy.16 = bf16[256,6144]{1,0:T(8,128)(2,1)} copy(bf16[256,6144]{1,0:T(8,128)(2,1)S(1)} %combine.1) | data formatting | bytes 6291456
Async XLA Ops:
  0.6 35.4 %copy-start.1 = (f32[6144]{0:T(1024)S(1)}, f32[6144]{0:T(1024)}, u32[]{:S(2)}) copy-start(f32[6144]{0:T(1024)} %param.23) | copy-start | bytes 73732
  36.0 1.5 %copy-start = (f32[3328,128]{1,0:T(8,128)S(1)}, f32[3328,128]{1,0:T(8,128)}, u32[]{:S(2)}) copy-start(f32[3328,128]{1,0:T(8,128)} %get-tuple-element.6) | copy-start | bytes 5111812
